TPU v7x, 128 devices: a whole 4x4x4 slice. The times are simulated.
128 devices in a mesh: wall: 64 (over z, y, x), stream: 2 (over core).
Axes of the slice: x: 4, y: 4, z: 4, core: 2. Of those that a mesh axis runs over, the one named last changes fastest.
Arguments:
- fields: float32 [5, 2, 12288, 2048], P(None, None, 'wall', 'stream'), may hold values from -5 to 5
- wall_velocity: float32 [2, 12288, 2048], P(None, 'wall', 'stream'), may hold values from -6 to 6
- diffusion: float32 [5], replicated, may hold values from 0.5 to 16
Outputs:
- tendency: float32 [5, 2, 12288, 2048], P(None, None, 'wall', 'stream')
- advanced: float32 [5, 2, 12288, 2048], P(None, None, 'wall', 'stream')
All inputs are finite; a program needn't handle non-finite values.
Results may differ from a plain program's by a relative error of at most 0.000094.
Values sent between devices are 32-bit elements; how exact they have to be, the bound alone decides.
No kernel may reach another device: no remote copies, remote signals or barrier semaphores. Data moves between devices by JAX's collectives and lax.ppermute only.
A program may use at most 128 MiB of HBM per device.

v0:
```python
import functools
import math

import jax
import jax.numpy as jnp
from jax import lax
from jax.experimental import pallas as pl
from jax.experimental.pallas import tpu as pltpu
from jax.sharding import PartitionSpec as P

time_step = 0.25
compact_alpha = 1.0 / 3.0
compact_near = 14.0 / 9.0
compact_far = 1.0 / 9.0
slope_ratio = (math.sqrt(1.0 - 4.0 * compact_alpha**2) - 1.0) / (2.0 * compact_alpha)
mix = 0.25 * compact_far / compact_alpha
rest = 0.5 * compact_near - mix
green = 1.0 / (1.0 + 2.0 * compact_alpha * slope_ratio)
kappa = rest * green * (slope_ratio - 1.0 / slope_ratio)
slope_gain = kappa * slope_ratio
slope_edge = -mix / slope_gain
tiny = 1.1754943508222875e-38
GROUP = 4
f32 = jnp.float32
MIB = 1 << 20


def params(mib):
    return pltpu.CompilerParams(vmem_limit_bytes=mib * MIB)


def lines(x):
    rows, cols = x.shape[-2:]
    y = x.reshape(-1, rows // 8, 8, cols // 128, 128)
    return jnp.swapaxes(y, 2, 3).reshape(-1, rows // 8, cols // 16, 128)


def unlines(y, shape):
    planes, tiles, wide, _ = y.shape
    y = y.reshape(planes, tiles, wide // 8, 8, 128)
    return jnp.swapaxes(y, 2, 3).reshape(shape)


def place():
    here = lax.axis_index("wall")
    return here, here == 0, here == lax.axis_size("wall") - 1


def edges_kernel(field_hbm, diffusion_hbm, field, sides, own, odd_out, even_out, coef, flag, rate, sems):
    planes, tiles = field.shape[0], field.shape[1]
    half = tiles // 2
    split = 4
    part = half // split
    copies = [pltpu.make_async_copy(field_hbm.at[p], field.at[p], sems.at[p]) for p in range(planes)]
    rates = pltpu.make_async_copy(diffusion_hbm, rate, sems.at[planes])
    rates.start()
    for copy in copies:
        copy.start()
    odd = place()[0] % 2 == 1

    def row(p, tile, r):
        return field[p, tile, pl.ds(r, 8, stride=8), :]

    rates.wait()
    longest = jnp.zeros((8, 128), f32)
    for k in range(rate.shape[0]):
        d = jnp.full((8, 128), rate[k])
        larger = 0.5 * (1.0 + 2.0 * d + jnp.sqrt(1.0 + 4.0 * d))
        ratio = d / larger
        log_ratio = jnp.log(ratio)
        weight = jnp.exp(8.0 * tiles * log_ratio)
        damp = 1.0 - ratio * ratio
        gain = time_step / larger
        for i, value in enumerate((ratio, gain, damp, weight, log_ratio, gain / damp)):
            coef[k, i] = value
        longest = jnp.maximum(longest, weight)
    flag[0] = (jnp.max(longest * longest) >= tiny).astype(jnp.int32)

    for p in range(planes):
        copies[p].wait()

        def step(t, carry, p=p):
            below, above = carry
            for r in range(8):
                below = [row(p, half + part * s + t, r) + slope_ratio * b for s, b in enumerate(below)]
                above = [row(p, part * s + part - 1 - t, 7 - r) + slope_ratio * a for s, a in enumerate(above)]
            return below, above

        zero = jnp.zeros((8, 128), f32)
        below, above = lax.fori_loop(0, part, step, ([zero] * split, [zero] * split))
        u, v = below[0], above[split - 1]
        jump = slope_ratio ** (8 * part)
        for s in range(1, split):
            u = below[s] + jump * u
            v = above[split - 1 - s] + jump * v
        top, bottom = row(p, tiles - 1, 7), row(p, 0, 0)
        for i, (a, b) in enumerate(((u, v), (top, bottom))):
            own[0, i, p] = a
            own[1, i, p] = b
            odd_out[i, p] = jnp.where(odd, a, b)
            even_out[i, p] = jnp.where(odd, b, a)
        for t in range(tiles):
            sides[0, p, t] = field[p, t, 0:8, :]
            sides[1, p, t] = field[p, t, 56:64, :]


def stencil():
    source = lax.broadcasted_iota(jnp.int32, (256, 256), 0) % 128
    target = lax.broadcasted_iota(jnp.int32, (256, 256), 1)
    offset = source - target % 128
    beyond = jnp.where(offset > 64, offset - 128, offset + 128)
    offset = jnp.where(target < 128, offset, beyond)
    size = jnp.abs(offset)
    value = jnp.where(size == 1, 45.0, jnp.where(size == 2, -9.0, jnp.where(size == 3, 1.0, 0.0)))
    return jnp.where(offset > 0, value, -value).astype(jnp.bfloat16)


def stream_kernel(field, sides, wall_hbm, out, wall, near, sem):
    planes, tiles = field.shape[0], field.shape[1]
    count = planes // 2
    copy = pltpu.make_async_copy(wall_hbm, wall, sem)
    copy.start()
    lane = lax.broadcasted_iota(jnp.int32, (8, 128), 1)
    matrix = stencil()
    group = GROUP

    def spread(x):
        high = x.astype(jnp.bfloat16)
        low = (x - high.astype(f32)).astype(jnp.bfloat16)
        return jnp.dot(jnp.concatenate([high, low], axis=1), matrix, preferred_element_type=f32)

    def outer(g, carry):
        p = g // 2
        side = g % 2
        x = sides[side, p].reshape(tiles * 8, 128)
        near[side, p] = spread(x)[:, 128:].reshape(tiles, 8, 128)
        return carry

    lax.fori_loop(0, 2 * planes, outer, 0)

    def body(g, carry):
        z = g // (tiles // group)
        first = (g % (tiles // group)) * group
        for k in range(count):
            p = k * 2 + z
            x = field[p, pl.ds(first, group)].reshape(group * 64, 128)
            both = spread(x)
            for t in range(group):
                tile = first + t
                part = [both[t * 64 + 8 * i : t * 64 + 8 * i + 8, 128:] for i in range(8)]
                part = [near[1, p, tile]] + part + [near[0, p, tile]]
                for i in range(8):
                    d = both[t * 64 + 8 * i : t * 64 + 8 * i + 8, :128]
                    d = d + jnp.where(lane < 64, part[i], part[i + 2])
                    speed = field[z, tile, 8 * i : 8 * i + 8, :] * (-1.0 / 60.0)
                    out[p, tile, 8 * i : 8 * i + 8, :] = speed * d
        return carry

    lax.fori_loop(0, 2 * tiles // group, body, 0)
    copy.wait()


def sweep_kernel(
    coef, field, stream, wall, own, odd_in, even_in, tend_hbm, adv, total, odd1, even1, odd2, even2, work, tend, sems
):
    planes, tiles = field.shape[0], field.shape[1]
    count = planes // 2
    ks = range(count)
    here, first, last_block = place()
    odd = here % 2 == 1
    pair = (here // 2) % 2 == 1
    image = mix / kappa

    def below(i, p):
        inner = jnp.where(odd, even_in[i, p], odd_in[i, p])
        edge = slope_ratio * own[1, 0, p] - image * own[1, 1, p] if i == 0 else jnp.zeros((8, 128), f32)
        return jnp.where(first, edge, inner)

    def above(i, p):
        inner = jnp.where(odd, odd_in[i, p], even_in[i, p])
        edge = slope_ratio * own[0, 0, p] - image * own[0, 1, p] if i == 0 else jnp.zeros((8, 128), f32)
        return jnp.where(last_block, edge, inner)

    def row(ref, p, tile, r):
        return ref[p, tile, pl.ds(r, 8, stride=8), :]

    ratio = [coef[k, 0] for k in ks]
    copies = []
    for z in range(2):
        at = [2 * k + z for k in ks]

        def rise(t, u):
            for r in range(8):
                for k in ks:
                    work[k, t, 8 * r : 8 * r + 8, :] = u[k]
                u = [row(field, at[k], t, r) + slope_ratio * u[k] for k in ks]
            return u

        lax.fori_loop(0, tiles, rise, [below(0, at[k]) for k in ks])

        ghost = [below(1, at[k]) for k in ks]

        def fall(i, carry):
            v, ahead, here, total = carry
            t = tiles - 1 - i
            for r in range(7, -1, -1):
                speed = row(wall, z, t, r) * (-slope_gain)
                if r > 0:
                    last = [row(field, at[k], t, r - 1) for k in ks]
                else:
                    before = jnp.maximum(t - 1, 0)
                    last = [jnp.where(t == 0, ghost[k], row(field, at[k], before, 7)) for k in ks]
                slope = [
                    (work[k, t, 8 * r : 8 * r + 8, :] - v[k]) + slope_edge * (last[k] - ahead[k]) for k in ks
                ]
                rate = [row(stream, at[k], t, r) + speed * slope[k] for k in ks]
                for k in ks:
                    tend[at[k], t, pl.ds(r, 8, stride=8), :] = rate[k]
                total = [(rate[k] + 8.0 * here[k]) + ratio[k] * total[k] for k in ks]
                for k in ks:
                    work[k, t, 8 * r : 8 * r + 8, :] = total[k]
                v = [here[k] + slope_ratio * v[k] for k in ks]
                ahead, here = here, last
            return v, ahead, here, total

        zero = jnp.zeros((8, 128), f32)
        start = (
            [above(0, at[k]) for k in ks],
            [above(1, at[k]) for k in ks],
            [row(field, at[k], tiles - 1, 7) for k in ks],
            [zero] * count,
        )
        bottom = lax.fori_loop(0, tiles, fall, start)[3]
        for k in ks:
            copy = pltpu.make_async_copy(tend.at[at[k]], tend_hbm.at[at[k]], sems.at[at[k]])
            copy.start()
            copies.append(copy)
        gain = [coef[k, 1] for k in ks]

        def settle(t, q):
            for r in range(8):
                q = [work[k, t, 8 * r : 8 * r + 8, :] + ratio[k] * q[k] for k in ks]
                for k in ks:
                    adv[at[k], t, pl.ds(r, 8, stride=8), :] = gain[k] * q[k] - row(field, at[k], t, r)
            return q

        top = lax.fori_loop(0, tiles, settle, [zero] * count)
        for k in ks:
            p = at[k]
            weight = coef[k, 3]
            up = coef[k, 2] * top[k] + weight * ratio[k] * bottom[k]
            down = bottom[k]
            total[0, p] = up
            total[1, p] = down
            send_up = jnp.where(first, up - weight * ratio[k] * down, up)
            send_down = jnp.where(last_block, down - weight * ratio[k] * up, down)
            odd1[p] = jnp.where(odd, send_up, send_down)
            even1[p] = jnp.where(odd, send_down, send_up)
            odd2[p] = jnp.where(pair, send_up, send_down)
            even2[p] = jnp.where(pair, send_down, send_up)
    for copy in copies:
        copy.wait()


def two_blocks(p, coef, total, odd1, even1, odd2, even2):
    here, first, last_block = place()
    odd = here % 2 == 1
    pair = (here // 2) % 2 == 1
    ratio, weight = coef[p // 2, 0], coef[p // 2, 3]
    low = jnp.where(odd, even1[p], odd1[p]) + weight * jnp.where(pair, even2[p], odd2[p])
    high = jnp.where(odd, odd1[p], even1[p]) + weight * jnp.where(pair, odd2[p], even2[p])
    end_low = -ratio * (total[1, p] + weight * high)
    end_high = -ratio * (total[0, p] + weight * low)
    return jnp.where(first, end_low, low), jnp.where(last_block, end_high, high)


def finish_kernel(coef, partial, total, odd1, even1, odd2, even2, out_hbm, out, sems):
    planes, tiles = partial.shape[0], partial.shape[1]
    line = lax.broadcasted_iota(jnp.int32, (8, 128), 0)
    copies = []
    for p in range(planes):
        k = p // 2
        ratio, log_ratio, scale = coef[k, 0], coef[k, 4], coef[k, 5]
        low, high = two_blocks(p, coef, total, odd1, even1, odd2, even2)
        low = scale * (ratio * total[1, p] + low)
        high = scale * high
        a = [jnp.broadcast_to(low[i : i + 1, :], (8, 128)) for i in range(8)]
        b = [jnp.broadcast_to(high[i : i + 1, :], (8, 128)) for i in range(8)]

        def body(t, carry, p=p, log_ratio=log_ratio, a=a, b=b):
            for s in range(2):
                tile = 2 * t + s
                at = (line + 8 * tile).astype(f32)
                fade = jnp.exp(log_ratio * (at + 1.0))
                grow = jnp.exp(log_ratio * (8.0 * tiles - at))
                for i in range(8):
                    piece = partial[p, tile, 8 * i : 8 * i + 8, :]
                    out[p, tile, 8 * i : 8 * i + 8, :] = piece + (fade * a[i] + grow * b[i])
            return carry

        lax.fori_loop(0, tiles // 2, body, 0)
        copy = pltpu.make_async_copy(out.at[p], out_hbm.at[p], sems.at[p])
        copy.start()
        copies.append(copy)
    for copy in copies:
        copy.wait()


def chain_kernel(coef, total, from_below, from_above, low_in, high_in, low_out, high_out, up_out, down_out):
    _, first, last_block = place()
    for p in range(total.shape[1]):
        ratio, weight = coef[p // 2, 0], coef[p // 2, 3]
        up, down = total[0, p], total[1, p]
        low = jnp.where(first, -ratio * (down + weight * high_in[p]), from_below[p])
        high = jnp.where(last_block, -ratio * (up + weight * low_in[p]), from_above[p])
        low_out[p] = low
        high_out[p] = high
        up_out[p] = up + weight * low
        down_out[p] = down + weight * high


def clear_kernel(*refs):
    for ref in refs:
        ref[...] = jnp.zeros(ref.shape, f32)


def chain_end_kernel(advanced, coef, total, odd1, even1, odd2, even2, low, high, out):
    planes, tiles = advanced.shape[0], advanced.shape[1]
    line = lax.broadcasted_iota(jnp.int32, (8, 128), 0)
    for p in range(planes):
        log_ratio, scale = coef[p // 2, 4], coef[p // 2, 5]
        near_low, near_high = two_blocks(p, coef, total, odd1, even1, odd2, even2)
        more_low = scale * (low[p] - near_low)
        more_high = scale * (high[p] - near_high)

        def body(tile, carry, p=p, log_ratio=log_ratio, more_low=more_low, more_high=more_high):
            at = (line + 8 * tile).astype(f32)
            fade = jnp.exp(log_ratio * (at + 1.0))
            grow = jnp.exp(log_ratio * (8.0 * tiles - at))
            for i in range(8):
                low_row = jnp.broadcast_to(more_low[i : i + 1, :], (8, 128))
                high_row = jnp.broadcast_to(more_high[i : i + 1, :], (8, 128))
                piece = advanced[p, tile, 8 * i : 8 * i + 8, :]
                out[p, tile, 8 * i : 8 * i + 8, :] = piece + (fade * low_row + grow * high_row)
            return carry

        lax.fori_loop(0, tiles, body, 0)


VMEM = pl.BlockSpec(memory_space=pltpu.VMEM)
SMEM = pl.BlockSpec(memory_space=pltpu.SMEM)
ANY = pl.BlockSpec(memory_space=pl.ANY)


def pairs(count, by, odd):
    found = []
    for a in range(count - by):
        if (a // by) % 2 == odd:
            found += [(a, a + by), (a + by, a)]
    return found


def exchange(odd, even, by):
    count = lax.axis_size("wall")
    return (
        lax.ppermute(odd, "wall", pairs(count, by, 1)),
        lax.ppermute(even, "wall", pairs(count, by, 0)),
    )


def whole_chain(advanced, coef, total, *arrived):
    count = lax.axis_size("wall")
    rise = [(i, i + 1) for i in range(count - 1)]
    fall = [(i + 1, i) for i in range(count - 1)]
    rows = jax.ShapeDtypeStruct(total.shape[1:], f32)

    def step(_, carry):
        low, high, up, down = carry
        return list(pl.pallas_call(
            chain_kernel,
            in_specs=[VMEM] * 6,
            out_specs=[VMEM] * 4,
            out_shape=[rows] * 4,
            compiler_params=params(2),
            name="chain",
        )(coef, total, lax.ppermute(up, "wall", rise), lax.ppermute(down, "wall", fall), low, high))

    start = list(pl.pallas_call(
        clear_kernel,
        out_specs=[VMEM] * 4,
        out_shape=[rows] * 4,
        compiler_params=params(2),
        name="chain_start",
    )())
    low, high, _, _ = lax.fori_loop(0, 2 * count, step, start)
    return pl.pallas_call(
        chain_end_kernel,
        in_specs=[VMEM] * 9,
        out_specs=VMEM,
        out_shape=jax.ShapeDtypeStruct(advanced.shape, f32),
        compiler_params=params(24),
        name="chain_end",
    )(advanced, coef, total, *arrived, low, high)


def on_device(fields, wall_velocity, diffusion):
    count, depth, height, width = fields.shape
    planes, tiles = count * depth, height // 8
    wide = width // 16
    shape = jax.ShapeDtypeStruct
    full = (planes, tiles, wide, 128)
    resident = pltpu.VMEM(full, f32)
    rows = shape((planes, 8, 128), f32)
    ends = shape((2, planes, 8, 128), f32)
    in_hbm = functools.partial(pltpu.with_memory_space_constraint, memory_space=pltpu.HBM)

    field, sides, own, odd, even, coef, flag = pl.pallas_call(
        edges_kernel,
        in_specs=[ANY, ANY],
        out_specs=[VMEM] * 6 + [SMEM],
        out_shape=[
            resident,
            shape((2, planes, tiles, 8, 128), f32),
            pltpu.VMEM((2, 2, planes, 8, 128), f32),
            ends,
            ends,
            pltpu.VMEM((count, 6, 8, 128), f32),
            shape((1,), jnp.int32),
        ],
        scratch_shapes=[pltpu.SMEM((count,), f32), pltpu.SemaphoreType.DMA((planes + 1,))],
        compiler_params=params(4),
        name="edges",
    )(in_hbm(lines(fields)), in_hbm(diffusion))
    sides = lax.ppermute(sides, "stream", [(0, 1), (1, 0)])
    odd, even = exchange(odd, even, 1)

    stream, wall = pl.pallas_call(
        stream_kernel,
        in_specs=[VMEM, VMEM, ANY],
        out_specs=[VMEM] * 2,
        out_shape=[resident, pltpu.VMEM((depth, tiles, wide, 128), f32)],
        scratch_shapes=[pltpu.VMEM((2, planes, tiles, 8, 128), f32), pltpu.SemaphoreType.DMA],
        compiler_params=params(8),
        cost_estimate=pl.CostEstimate(flops=4_000_000_000, transcendentals=0, bytes_accessed=0),
        name="streamwise",
    )(field, sides, in_hbm(lines(wall_velocity)))

    tendency, partial, total, *sent = pl.pallas_call(
        sweep_kernel,
        in_specs=[VMEM] * 7,
        out_specs=[ANY] + [VMEM] * 6,
        out_shape=[shape(full, f32), resident, pltpu.VMEM((2, planes, 8, 128), f32)] + [rows] * 4,
        scratch_shapes=[
            pltpu.VMEM((count, tiles, wide, 128), f32),
            pltpu.VMEM(full, f32),
            pltpu.SemaphoreType.DMA((planes,)),
        ],
        compiler_params=params(14),
        name="sweeps",
    )(coef, field, stream, wall, own, odd, even)

    odd1, even1, odd2, even2 = sent
    far = exchange(odd2, even2, 2)
    near = exchange(odd1, even1, 1)
    arrived = [*near, *far]

    advanced = pl.pallas_call(
        finish_kernel,
        in_specs=[VMEM] * 7,
        out_specs=ANY,
        out_shape=shape(full, f32),
        scratch_shapes=[pltpu.VMEM(full, f32), pltpu.SemaphoreType.DMA((planes,))],
        compiler_params=params(10),
        name="finish",
    )(coef, partial, total, *arrived)
    advanced = lax.cond(flag[0] != 0, whole_chain, lambda x, *_: x, advanced, coef, total, *arrived)
    return unlines(tendency, fields.shape), unlines(advanced, fields.shape)


def solution(mesh):
    tall = P(None, None, "wall", "stream")
    return jax.shard_map(
        on_device,
        mesh=mesh,
        in_specs=(tall, P(None, "wall", "stream"), P()),
        out_specs=(tall, tall),
        check_vma=False,
    )
```

profile of v0, /device:TPU:96, one launch (start us, length us, event | category | flops | bytes accessed | tf_op | source)
XLA Modules:
  0.0 51.1 jit_solution(3232668767288331240)
XLA Ops:
  0.6 4.0 %edges.1 = (f32[10,24,64,128]{3,2,1,0:T(8,128)S(1)}, f32[2,10,24,8,128]{4,3,2,1,0:T(8,128)S(1)}, f32[2,2,10,8,128]{4,3,2,1,0:T(8,128)S(1)}, f32[2,10,8,128]{3,2,...) custom-call(f32[10,24,64,128]{3,2,1,0:T(8,128)} %bitcast.22, f32[5]{0:T(128)} %diffusion_hbm.1), custom_call_target="tpu_custom_call" | custom-call | tf_op jit(solution)/shard_map/edges/pallas_call | solution.py:417
  4.7 0.1 collective-permute-start.2
  4.7 7.0 %collective-permute-start.3 = (f32[2,10,8,128]{3,2,1,0:T(8,128)S(1)}, f32[2,10,8,128]{3,2,1,0:T(8,128)S(1)}, u32[]{:S(2)}, u32[]{:S(2)}) collective-permute-start(f32[2,10,8,128]{3,2,1,0:T(8,128)S(1)} %get-tuple-element.95), channel_id=1, source_target_pairs={{2,4},{4,2},{6,8},{8,6},{10,12},{12,10},{14,16},{16,14},{18,20},{2... | collective-permute-start | bytes 245768 | tf_op jit(solution)/shard_map/ppermute | solution.py:366
  11.7 0.1 collective-permute-start.4
  11.8 0.0 collective-permute-done.2.sides
  11.8 8.0 %streamwise.1 = (f32[10,24,64,128]{3,2,1,0:T(8,128)S(1)}, f32[2,24,64,128]{3,2,1,0:T(8,128)S(1)}) custom-call(f32[10,24,64,128]{3,2,1,0:T(8,128)S(1)} %get-tuple-element.90.field, f32[2,10,24,8,128]{4,3,2,1,0:T(8,128)S(1)} %collective-permute-done.2.sides, f32[2,24,64,128]{3,2,1,0:T(8,128)} %bitcast.24), custom_call_target="tpu_custom_call" | custom-call | flops 4000000000 | tf_op jit(solution)/shard_map/streamwise/pallas_call | solution.py:437
  19.8 0.0 collective-permute-done.3.odd_in
  19.8 0.0 collective-permute-done.4.even_in
  19.8 10.2 %sweeps.1 = (f32[10,24,64,128]{3,2,1,0:T(8,128)}, f32[10,24,64,128]{3,2,1,0:T(8,128)S(1)}, f32[2,10,8,128]{3,2,1,0:T(8,128)S(1)}, f32[10,8,128]{2,1,0:T(8,128)S(...) custom-call(f32[5,6,8,128]{3,2,1,0:T(8,128)S(1)} %get-tuple-element.89.coef, ...), custom_call_target="tpu_custom_call" | custom-call | tf_op jit(solution)/shard_map/sweeps/pallas_call | solution.py:448
  30.0 3.9 %collective-permute-start.5 = (f32[10,8,128]{2,1,0:T(8,128)S(1)}, f32[10,8,128]{2,1,0:T(8,128)S(1)}, u32[]{:S(2)}, u32[]{:S(2)}) collective-permute-start(f32[10,8,128]{2,1,0:T(8,128)S(1)} %get-tuple-element.101), channel_id=1, source_target_pairs={{2,4},{4,2},{6,8},{8,6},{10,12},{12,10},{14,16},{16,14},{18,20},{2... | collective-permute-start | bytes 122888 | tf_op jit(solution)/shard_map/ppermute | solution.py:366
  33.9 0.1 collective-permute-start.6
  34.1 7.6 %collective-permute-start.7 = (f32[10,8,128]{2,1,0:T(8,128)S(1)}, f32[10,8,128]{2,1,0:T(8,128)S(1)}, u32[]{:S(2)}, u32[]{:S(2)}) collective-permute-start(f32[10,8,128]{2,1,0:T(8,128)S(1)} %get-tuple-element.103), channel_id=1, source_target_pairs={{4,8},{8,4},{6,10},{10,6},{12,16},{16,12},{14,18},{18,14},{20,24},... | collective-permute-start | bytes 122888 | tf_op jit(solution)/shard_map/ppermute | solution.py:366
  41.7 0.1 collective-permute-start.8
  42.4 0.0 collective-permute-done.5.odd1
  42.4 0.0 collective-permute-done.6.even1
  42.4 2.0 %collective-permute-done.7.odd2 = f32[10,8,128]{2,1,0:T(8,128)S(1)} collective-permute-done((f32[10,8,128]{2,1,0:T(8,128)S(1)}, f32[10,8,128]{2,1,0:T(8,128)S(1)}, u32[]{:S(2)}, u32[]{:S(2)}) %collective-permute-start.7) | collective-permute-done | bytes 40992 | tf_op jit(solution)/shard_map/ppermute | solution.py:366
  44.5 2.8 %collective-permute-done.8.even2 = f32[10,8,128]{2,1,0:T(8,128)S(1)} collective-permute-done((f32[10,8,128]{2,1,0:T(8,128)S(1)}, f32[10,8,128]{2,1,0:T(8,128)S(1)}, u32[]{:S(2)}, u32[]{:S(2)}) %collective-permute-start.8) | collective-permute-done | bytes 40992 | tf_op jit(solution)/shard_map/ppermute | solution.py:367
  47.2 3.8 %finish.1 = f32[10,24,64,128]{3,2,1,0:T(8,128)} custom-call(f32[5,6,8,128]{3,2,1,0:T(8,128)S(1)} %get-tuple-element.89.coef, f32[10,24,64,128]{3,2,1,0:T(8,128)S(1)} %get-tuple-element.99.partial, f32[2,10,8,128]{3,2,1,0:T(8,128)S(1)} %get-tuple-element.100.total, f32[10,8,128]{2,1,0:T(8,128)S(1)} %collective-permute-done.5.odd1, ...), custom_call_target="tpu_custom_call" | custom-call | tf_op jit(solution)/shard_map/finish/pallas_call | solution.py:467
  (1 shorter events, 0.0 us)
Async XLA Ops:
  4.7 7.2 %collective-permute-start.2 = (f32[2,10,24,8,128]{4,3,2,1,0:T(8,128)S(1)}, f32[2,10,24,8,128]{4,3,2,1,0:T(8,128)S(1)}, u32[]{:S(2)}, u32[]{:S(2)}) collective-permute-start(f32[2,10,24,8,128]{4,3,2,1,0:T(8,128)S(1)} %get-tuple-element.91), channel_id=1, source_target_pairs={{0,1},{1,0},{2,3},{3,2},{4,5},{5,4},{6,7},{7,6},{8,9},{9,8},{10,11... | collective-permute-start | bytes 5898248 | tf_op jit(solution)/shard_map/ppermute | solution.py:434
  4.7 15.1 %collective-permute-start.3 = (f32[2,10,8,128]{3,2,1,0:T(8,128)S(1)}, f32[2,10,8,128]{3,2,1,0:T(8,128)S(1)}, u32[]{:S(2)}, u32[]{:S(2)}) collective-permute-start(f32[2,10,8,128]{3,2,1,0:T(8,128)S(1)} %get-tuple-element.95), channel_id=1, source_target_pairs={{2,4},{4,2},{6,8},{8,6},{10,12},{12,10},{14,16},{16,14},{18,20},{2... | collective-permute-start | bytes 245768 | tf_op jit(solution)/shard_map/ppermute | solution.py:366
  11.7 8.1 %collective-permute-start.4 = (f32[2,10,8,128]{3,2,1,0:T(8,128)S(1)}, f32[2,10,8,128]{3,2,1,0:T(8,128)S(1)}, u32[]{:S(2)}, u32[]{:S(2)}) collective-permute-start(f32[2,10,8,128]{3,2,1,0:T(8,128)S(1)} %get-tuple-element.96), channel_id=1, source_target_pairs={{0,2},{2,0},{4,6},{6,4},{8,10},{10,8},{12,14},{14,12},{16,18},{18,... | collective-permute-start | bytes 245768 | tf_op jit(solution)/shard_map/ppermute | solution.py:367
  30.0 12.4 %collective-permute-start.5 = (f32[10,8,128]{2,1,0:T(8,128)S(1)}, f32[10,8,128]{2,1,0:T(8,128)S(1)}, u32[]{:S(2)}, u32[]{:S(2)}) collective-permute-start(f32[10,8,128]{2,1,0:T(8,128)S(1)} %get-tuple-element.101), channel_id=1, source_target_pairs={{2,4},{4,2},{6,8},{8,6},{10,12},{12,10},{14,16},{16,14},{18,20},{2... | collective-permute-start | bytes 122888 | tf_op jit(solution)/shard_map/ppermute | solution.py:366
  33.9 8.5 %collective-permute-start.6 = (f32[10,8,128]{2,1,0:T(8,128)S(1)}, f32[10,8,128]{2,1,0:T(8,128)S(1)}, u32[]{:S(2)}, u32[]{:S(2)}) collective-permute-start(f32[10,8,128]{2,1,0:T(8,128)S(1)} %get-tuple-element.102), channel_id=1, source_target_pairs={{0,2},{2,0},{4,6},{6,4},{8,10},{10,8},{12,14},{14,12},{16,18},{18,... | collective-permute-start | bytes 122888 | tf_op jit(solution)/shard_map/ppermute | solution.py:367
  34.1 10.4 %collective-permute-start.7 = (f32[10,8,128]{2,1,0:T(8,128)S(1)}, f32[10,8,128]{2,1,0:T(8,128)S(1)}, u32[]{:S(2)}, u32[]{:S(2)}) collective-permute-start(f32[10,8,128]{2,1,0:T(8,128)S(1)} %get-tuple-element.103), channel_id=1, source_target_pairs={{4,8},{8,4},{6,10},{10,6},{12,16},{16,12},{14,18},{18,14},{20,24},... | collective-permute-start | bytes 122888 | tf_op jit(solution)/shard_map/ppermute | solution.py:366
  41.7 5.6 %collective-permute-start.8 = (f32[10,8,128]{2,1,0:T(8,128)S(1)}, f32[10,8,128]{2,1,0:T(8,128)S(1)}, u32[]{:S(2)}, u32[]{:S(2)}) collective-permute-start(f32[10,8,128]{2,1,0:T(8,128)S(1)} %get-tuple-element.104), channel_id=1, source_target_pairs={{0,4},{4,0},{2,6},{6,2},{8,12},{12,8},{10,14},{14,10},{16,20},{20,... | collective-permute-start | bytes 122888 | tf_op jit(solution)/shard_map/ppermute | solution.py:367
where the time goes:
time: 51.3 us; the launch traced here: 51.1 us
  Pallas kernels  26.1 us (51%)
  starting transfers between devices  18.8 us (37%)
  waiting for transfers between devices  4.84 us (9%)
  between operations  1.4 us (3%)
    ppermute x3, starting transfers between devices, exchange(): lax.ppermute(odd, 'wall', pairs(count, by, 1))  18.4 us
    pallas_call x1, Pallas kernels, on_device(): pl.pallas_call(sweep_kernel, in_specs=[VMEM] * 7, out_specs=[ANY] + [VMEM...  10.2 us
    pallas_call x1, Pallas kernels, on_device(): pl.pallas_call(stream_kernel, in_specs=[VMEM, VMEM, ANY], out_specs=[VMEM...  8 us
    pallas_call x1, Pallas kernels, on_device(): pl.pallas_call(edges_kernel, in_specs=[ANY, ANY], out_specs=[VMEM] * 6 +...  4.02 us
    pallas_call x1, Pallas kernels, on_device(): pl.pallas_call(finish_kernel, in_specs=[VMEM] * 7, out_specs=ANY, out_sha...  3.84 us
    ppermute x3, waiting for transfers between devices, exchange(): lax.ppermute(even, 'wall', pairs(count, by, 0))  2.79 us
    ppermute x3, waiting for transfers between devices, exchange(): lax.ppermute(odd, 'wall', pairs(count, by, 1))  2.04 us
  transfers between devices with their start and end apart: 7, of which 2 were waited for; matrix products, arithmetic and copies ran while one was open for 0% of the time, Pallas kernels for 16%

commit v1 on v0

v1 whole, which is shorter than its diff:
```python
import functools
import math

import jax
import jax.numpy as jnp
from jax import lax
from jax.experimental import pallas as pl
from jax.experimental.pallas import tpu as pltpu
from jax.sharding import PartitionSpec as P

time_step = 0.25
compact_alpha = 1.0 / 3.0
compact_near = 14.0 / 9.0
compact_far = 1.0 / 9.0
slope_ratio = (math.sqrt(1.0 - 4.0 * compact_alpha**2) - 1.0) / (2.0 * compact_alpha)
mix = 0.25 * compact_far / compact_alpha
rest = 0.5 * compact_near - mix
green = 1.0 / (1.0 + 2.0 * compact_alpha * slope_ratio)
kappa = rest * green * (slope_ratio - 1.0 / slope_ratio)
slope_gain = kappa * slope_ratio
slope_edge = -mix / slope_gain
tiny = 1.1754943508222875e-38
SPLIT = 6
f32 = jnp.float32
MIB = 1 << 20


def params(mib):
    return pltpu.CompilerParams(vmem_limit_bytes=mib * MIB)


def lines(x):
    rows, cols = x.shape[-2:]
    y = x.reshape(-1, rows // 8, 8, cols // 128, 128)
    return jnp.swapaxes(y, 2, 3)[:, :, :, :, None, :]


def unlines(y, shape):
    return jnp.swapaxes(y[:, :, :, :, 0, :], 2, 3).reshape(shape)


def load_rows(hbm, rows, sems, p):
    return [
        pltpu.make_async_copy(hbm.at[p, :, :, r, 0], rows.at[p, :, r], sems.at[p, r]) for r in range(8)
    ]


def store_rows(rows, hbm, sems, p):
    return [
        pltpu.make_async_copy(rows.at[p, :, r], hbm.at[p, :, :, r, 0], sems.at[p, r]) for r in range(8)
    ]


def place():
    here = lax.axis_index("wall")
    return here, here == 0, here == lax.axis_size("wall") - 1


def edges_kernel(field_hbm, diffusion_hbm, field, sides, own, odd_out, even_out, coef, fading, flag, rate, sems, sem):
    planes, tiles = field.shape[0], field.shape[1]
    half = tiles // 2
    split = SPLIT
    part = half // split
    rates = pltpu.make_async_copy(diffusion_hbm, rate, sem)
    rates.start()
    copies = [load_rows(field_hbm, field, sems, p) for p in range(planes)]
    for copy in sum(copies, []):
        copy.start()
    odd = place()[0] % 2 == 1

    def coefficients():
        rates.wait()
        longest = jnp.zeros((8, 128), f32)
        for k in range(rate.shape[0]):
            d = jnp.full((8, 128), rate[k])
            larger = 0.5 * (1.0 + 2.0 * d + jnp.sqrt(1.0 + 4.0 * d))
            ratio = d / larger
            log_ratio = jnp.log(ratio)
            weight = jnp.exp(8.0 * tiles * log_ratio)
            damp = 1.0 - ratio * ratio
            gain = time_step / larger
            for i, value in enumerate((ratio, gain, damp, weight, log_ratio, gain / damp)):
                coef[k, i] = value
            longest = jnp.maximum(longest, weight)
            line = lax.broadcasted_iota(jnp.int32, (8, 128), 0).astype(f32) + 1.0
            for tile in range(tiles):
                fading[k, tile] = jnp.exp(log_ratio * (line + 8.0 * tile))
        flag[0] = (jnp.max(longest * longest) >= tiny).astype(jnp.int32)

    for p in range(planes):
        for copy in copies[p]:
            copy.wait()
        if p == planes // 2:
            coefficients()

        def step(t, carry, p=p):
            below, above = carry
            for r in range(8):
                below = [field[p, half + part * s + t, r] + slope_ratio * b for s, b in enumerate(below)]
                above = [field[p, part * s + part - 1 - t, 7 - r] + slope_ratio * a for s, a in enumerate(above)]
            return below, above

        zero = jnp.zeros((8, 128), f32)
        below, above = lax.fori_loop(0, part, step, ([zero] * split, [zero] * split))
        u, v = below[0], above[split - 1]
        jump = slope_ratio ** (8 * part)
        for s in range(1, split):
            u = below[s] + jump * u
            v = above[split - 1 - s] + jump * v
        top, bottom = field[p, tiles - 1, 7], field[p, 0, 0]
        for i, (a, b) in enumerate(((u, v), (top, bottom))):
            own[0, i, p] = a
            own[1, i, p] = b
            odd_out[i, p] = jnp.where(odd, a, b)
            even_out[i, p] = jnp.where(odd, b, a)
        flat = field.at[p].reshape(tiles * 64, 128)
        for t in range(tiles):
            sides[0, p, t] = flat[pl.ds(64 * t, 8, stride=8), :]
            sides[1, p, t] = flat[pl.ds(64 * t + 7, 8, stride=8), :]


def stencil():
    source = lax.broadcasted_iota(jnp.int32, (256, 256), 0) % 128
    target = lax.broadcasted_iota(jnp.int32, (256, 256), 1)
    offset = source - target % 128
    beyond = jnp.where(offset > 64, offset - 128, offset + 128)
    offset = jnp.where(target < 128, offset, beyond)
    size = jnp.abs(offset)
    value = jnp.where(size == 1, 45.0, jnp.where(size == 2, -9.0, jnp.where(size == 3, 1.0, 0.0)))
    return jnp.where(offset > 0, value, -value).astype(jnp.bfloat16)


def stream_kernel(field, sides, wall_hbm, out, wall, near, sems):
    planes, tiles = field.shape[0], field.shape[1]
    copies = sum([load_rows(wall_hbm, wall, sems, z) for z in range(wall.shape[0])], [])
    for copy in copies:
        copy.start()
    lane = lax.broadcasted_iota(jnp.int32, (8, 128), 1)
    piece = lax.broadcasted_iota(jnp.int32, (8, 128), 0)
    left = lane < 64
    outer = ((piece == 0) & left) | ((piece == 7) & (lane >= 64))
    matrix = stencil()

    def spread(x, columns):
        high = x.astype(jnp.bfloat16)
        low = (x - high.astype(f32)).astype(jnp.bfloat16)
        return jnp.dot(jnp.concatenate([high, low], axis=1), columns, preferred_element_type=f32)

    before = spread(sides[1].reshape(planes * tiles * 8, 128), matrix[:, 128:])
    after = spread(sides[0].reshape(planes * tiles * 8, 128), matrix[:, 128:])
    first = lax.broadcasted_iota(jnp.int32, before.shape, 1) < 64
    near[...] = jnp.where(first, before, after).reshape(planes, tiles, 8, 128)

    def body(p, carry):
        both = spread(field[p].reshape(tiles * 64, 128), matrix)
        for tile in range(tiles):
            for r in range(8):
                at = tile * 64 + 8 * r
                part = both[at : at + 8, 128:]
                part = jnp.where(left, pltpu.roll(part, 1, 0), pltpu.roll(part, 7, 0))
                part = jnp.where(outer, jnp.broadcast_to(near[p, tile, r : r + 1, :], (8, 128)), part)
                speed = field[p % 2, tile, r] * (-1.0 / 60.0)
                out[p, tile, r] = speed * (both[at : at + 8, :128] + part)
        return carry

    lax.fori_loop(0, planes, body, 0)
    for copy in copies:
        copy.wait()


def sweep_kernel(
    coef, field, stream, wall, own, odd_in, even_in, tend_hbm, adv, total, odd1, even1, odd2, even2, work, tend, sems
):
    planes, tiles = field.shape[0], field.shape[1]
    count = planes // 2
    ks = range(count)
    here, first, last_block = place()
    odd = here % 2 == 1
    pair = (here // 2) % 2 == 1
    image = mix / kappa

    def below(i, p):
        inner = jnp.where(odd, even_in[i, p], odd_in[i, p])
        edge = slope_ratio * own[1, 0, p] - image * own[1, 1, p] if i == 0 else jnp.zeros((8, 128), f32)
        return jnp.where(first, edge, inner)

    def above(i, p):
        inner = jnp.where(odd, odd_in[i, p], even_in[i, p])
        edge = slope_ratio * own[0, 0, p] - image * own[0, 1, p] if i == 0 else jnp.zeros((8, 128), f32)
        return jnp.where(last_block, edge, inner)

    every = range(planes)
    ratio = [coef[k, 0] for k in ks]
    copies = []
    zero = jnp.zeros((8, 128), f32)

    def rise(t, u):
        for r in range(8):
            for p in every:
                work[p, t, r] = u[p]
            u = [field[p, t, r] + slope_ratio * u[p] for p in every]
        return u

    lax.fori_loop(0, tiles, rise, [below(0, p) for p in every])

    bottom = {}
    for z in range(2):
        at = [2 * k + z for k in ks]
        ghost = [below(1, at[k]) for k in ks]

        def fall(i, carry, z=z, at=at, ghost=ghost):
            v, ahead, here, total = carry
            t = tiles - 1 - i
            for r in range(7, -1, -1):
                speed = wall[z, t, r] * (-slope_gain)
                if r > 0:
                    last = [field[at[k], t, r - 1] for k in ks]
                else:
                    before = jnp.maximum(t - 1, 0)
                    last = [jnp.where(t == 0, ghost[k], field[at[k], before, 7]) for k in ks]
                slope = [
                    (work[at[k], t, r] - v[k]) + slope_edge * (last[k] - ahead[k]) for k in ks
                ]
                rate = [stream[at[k], t, r] + speed * slope[k] for k in ks]
                for k in ks:
                    tend[at[k], t, r] = rate[k]
                total = [(rate[k] + 8.0 * here[k]) + ratio[k] * total[k] for k in ks]
                for k in ks:
                    work[at[k], t, r] = total[k]
                v = [here[k] + slope_ratio * v[k] for k in ks]
                ahead, here = here, last
            return v, ahead, here, total

        start = (
            [above(0, at[k]) for k in ks],
            [above(1, at[k]) for k in ks],
            [field[at[k], tiles - 1, 7] for k in ks],
            [zero] * count,
        )
        lowest = lax.fori_loop(0, tiles, fall, start)[3]
        for k in ks:
            bottom[at[k]] = lowest[k]
            for copy in store_rows(tend, tend_hbm, sems, at[k]):
                copy.start()
                copies.append(copy)
    gain = [coef[k, 1] for k in ks]

    def settle(t, q):
        for r in range(8):
            q = [work[p, t, r] + ratio[p // 2] * q[p] for p in every]
            for p in every:
                adv[p, t, r] = gain[p // 2] * q[p] - field[p, t, r]
        return q

    top = lax.fori_loop(0, tiles, settle, [zero] * planes)
    for p in every:
        weight, step = coef[p // 2, 3], ratio[p // 2]
        up = coef[p // 2, 2] * top[p] + weight * step * bottom[p]
        down = bottom[p]
        total[0, p] = up
        total[1, p] = down
        send_up = jnp.where(first, up - weight * step * down, up)
        send_down = jnp.where(last_block, down - weight * step * up, down)
        odd1[p] = jnp.where(odd, send_up, send_down)
        even1[p] = jnp.where(odd, send_down, send_up)
        odd2[p] = jnp.where(pair, send_up, send_down)
        even2[p] = jnp.where(pair, send_down, send_up)
    for copy in copies:
        copy.wait()


def two_blocks(p, coef, total, odd1, even1, odd2, even2):
    here, first, last_block = place()
    odd = here % 2 == 1
    pair = (here // 2) % 2 == 1
    ratio, weight = coef[p // 2, 0], coef[p // 2, 3]
    low = jnp.where(odd, even1[p], odd1[p]) + weight * jnp.where(pair, even2[p], odd2[p])
    high = jnp.where(odd, odd1[p], even1[p]) + weight * jnp.where(pair, odd2[p], even2[p])
    end_low = -ratio * (total[1, p] + weight * high)
    end_high = -ratio * (total[0, p] + weight * low)
    return jnp.where(first, end_low, low), jnp.where(last_block, end_high, high)


def add_ends(k, lows, highs, fading, source, target):
    tiles = source.shape[1]

    def body(t, carry):
        for r in range(8):
            fade = jnp.broadcast_to(fading[k, t, r : r + 1, :], (8, 128))
            grow = jnp.broadcast_to(fading[k, tiles - 1 - t, 7 - r : 8 - r, :], (8, 128))
            for p, low, high in zip((2 * k, 2 * k + 1), lows, highs):
                target[p, t, r] = source[p, t, r] + (fade * low + grow * high)
        return carry

    lax.fori_loop(0, tiles, body, 0)


def finish_kernel(coef, fading, partial, total, odd1, even1, odd2, even2, out_hbm, out, sems):
    copies = []
    for k in range(coef.shape[0]):
        ratio, scale = coef[k, 0], coef[k, 5]
        lows, highs = [], []
        for p in (2 * k, 2 * k + 1):
            low, high = two_blocks(p, coef, total, odd1, even1, odd2, even2)
            lows.append(scale * (ratio * total[1, p] + low))
            highs.append(scale * high)
        add_ends(k, lows, highs, fading, partial, out)
        for p in (2 * k, 2 * k + 1):
            for copy in store_rows(out, out_hbm, sems, p):
                copy.start()
                copies.append(copy)
    for copy in copies:
        copy.wait()


def chain_kernel(coef, total, from_below, from_above, low_in, high_in, low_out, high_out, up_out, down_out):
    _, first, last_block = place()
    for p in range(total.shape[1]):
        ratio, weight = coef[p // 2, 0], coef[p // 2, 3]
        up, down = total[0, p], total[1, p]
        low = jnp.where(first, -ratio * (down + weight * high_in[p]), from_below[p])
        high = jnp.where(last_block, -ratio * (up + weight * low_in[p]), from_above[p])
        low_out[p] = low
        high_out[p] = high
        up_out[p] = up + weight * low
        down_out[p] = down + weight * high


def clear_kernel(*refs):
    for ref in refs:
        ref[...] = jnp.zeros(ref.shape, f32)


def chain_end_kernel(
    advanced_hbm, coef, fading, total, odd1, even1, odd2, even2, low, high, out_hbm, before, after, loads, stores
):
    for k in range(coef.shape[0]):
        pair = (2 * k, 2 * k + 1)
        scale = coef[k, 5]
        lows, highs = [], []
        for p in pair:
            near_low, near_high = two_blocks(p, coef, total, odd1, even1, odd2, even2)
            lows.append(scale * (low[p] - near_low))
            highs.append(scale * (high[p] - near_high))
        copies = sum([load_rows(advanced_hbm, before, loads, p) for p in pair], [])
        for copy in copies:
            copy.start()
        for copy in copies:
            copy.wait()
        add_ends(k, lows, highs, fading, before, after)
        copies = sum([store_rows(after, out_hbm, stores, p) for p in pair], [])
        for copy in copies:
            copy.start()
        for copy in copies:
            copy.wait()


VMEM = pl.BlockSpec(memory_space=pltpu.VMEM)
SMEM = pl.BlockSpec(memory_space=pltpu.SMEM)
ANY = pl.BlockSpec(memory_space=pl.ANY)


def pairs(count, by, odd):
    found = []
    for a in range(count - by):
        if (a // by) % 2 == odd:
            found += [(a, a + by), (a + by, a)]
    return found


def row_shape(shape):
    planes, tiles = shape[:2]
    return (planes, tiles, 8, 8, 128)


def exchange(odd, even, by):
    count = lax.axis_size("wall")
    return (
        lax.ppermute(odd, "wall", pairs(count, by, 1)),
        lax.ppermute(even, "wall", pairs(count, by, 0)),
    )


def whole_chain(advanced, coef, fading, total, *arrived):
    count = lax.axis_size("wall")
    rise = [(i, i + 1) for i in range(count - 1)]
    fall = [(i + 1, i) for i in range(count - 1)]
    rows = jax.ShapeDtypeStruct(total.shape[1:], f32)
    planes = advanced.shape[0]

    def step(_, carry):
        low, high, up, down = carry
        return list(pl.pallas_call(
            chain_kernel,
            in_specs=[VMEM] * 6,
            out_specs=[VMEM] * 4,
            out_shape=[rows] * 4,
            compiler_params=params(2),
            name="chain",
        )(coef, total, lax.ppermute(up, "wall", rise), lax.ppermute(down, "wall", fall), low, high))

    start = list(pl.pallas_call(
        clear_kernel,
        out_specs=[VMEM] * 4,
        out_shape=[rows] * 4,
        compiler_params=params(2),
        name="chain_start",
    )())
    low, high, _, _ = lax.fori_loop(0, 2 * count, step, start)
    return pl.pallas_call(
        chain_end_kernel,
        in_specs=[ANY] + [VMEM] * 9,
        out_specs=ANY,
        out_shape=jax.ShapeDtypeStruct(advanced.shape, f32),
        scratch_shapes=[pltpu.VMEM(row_shape(advanced.shape), f32)] * 2 + [pltpu.SemaphoreType.DMA((planes, 8))] * 2,
        compiler_params=params(18),
        name="chain_end",
    )(advanced, coef, fading, total, *arrived, low, high)


def on_device(fields, wall_velocity, diffusion):
    count, depth, height, width = fields.shape
    planes, tiles = count * depth, height // 8
    shape = jax.ShapeDtypeStruct
    source, wall_source = lines(fields), lines(wall_velocity)
    full = row_shape(source.shape)
    resident = pltpu.VMEM(full, f32)
    rows = shape((planes, 8, 128), f32)
    ends = shape((2, planes, 8, 128), f32)
    in_hbm = functools.partial(pltpu.with_memory_space_constraint, memory_space=pltpu.HBM)
    plane_sems = pltpu.SemaphoreType.DMA((planes, 8))

    field, sides, own, odd, even, coef, fading, flag = pl.pallas_call(
        edges_kernel,
        in_specs=[ANY, ANY],
        out_specs=[VMEM] * 7 + [SMEM],
        out_shape=[
            resident,
            shape((2, planes, tiles, 8, 128), f32),
            pltpu.VMEM((2, 2, planes, 8, 128), f32),
            ends,
            ends,
            pltpu.VMEM((count, 6, 8, 128), f32),
            pltpu.VMEM((count, tiles, 8, 128), f32),
            shape((1,), jnp.int32),
        ],
        scratch_shapes=[pltpu.SMEM((count,), f32), plane_sems, pltpu.SemaphoreType.DMA],
        compiler_params=params(4),
        name="edges",
    )(in_hbm(source), in_hbm(diffusion))
    sides = lax.ppermute(sides, "stream", [(0, 1), (1, 0)])
    odd, even = exchange(odd, even, 1)

    stream, wall = pl.pallas_call(
        stream_kernel,
        in_specs=[VMEM, VMEM, ANY],
        out_specs=[VMEM] * 2,
        out_shape=[resident, pltpu.VMEM(row_shape(wall_source.shape), f32)],
        scratch_shapes=[pltpu.VMEM((planes, tiles, 8, 128), f32), pltpu.SemaphoreType.DMA((depth, 8))],
        compiler_params=params(12),
        cost_estimate=pl.CostEstimate(flops=4_000_000_000, transcendentals=0, bytes_accessed=0),
        name="streamwise",
    )(field, sides, in_hbm(wall_source))

    tendency, partial, total, *sent = pl.pallas_call(
        sweep_kernel,
        in_specs=[VMEM] * 7,
        out_specs=[ANY] + [VMEM] * 6,
        out_shape=[shape(source.shape, f32), resident, pltpu.VMEM((2, planes, 8, 128), f32)] + [rows] * 4,
        scratch_shapes=[pltpu.VMEM(full, f32), pltpu.VMEM(full, f32), plane_sems],
        compiler_params=params(18),
        name="sweeps",
    )(coef, field, stream, wall, own, odd, even)

    odd1, even1, odd2, even2 = sent
    far = exchange(odd2, even2, 2)
    near = exchange(odd1, even1, 1)
    arrived = [*near, *far]

    advanced = pl.pallas_call(
        finish_kernel,
        in_specs=[VMEM] * 8,
        out_specs=ANY,
        out_shape=shape(source.shape, f32),
        scratch_shapes=[pltpu.VMEM(full, f32), plane_sems],
        compiler_params=params(10),
        name="finish",
    )(coef, fading, partial, total, *arrived)
    advanced = lax.cond(flag[0] != 0, whole_chain, lambda x, *_: x, advanced, coef, fading, total, *arrived)
    return unlines(tendency, fields.shape), unlines(advanced, fields.shape)


def solution(mesh):
    tall = P(None, None, "wall", "stream")
    return jax.shard_map(
        on_device,
        mesh=mesh,
        in_specs=(tall, P(None, "wall", "stream"), P()),
        out_specs=(tall, tall),
        check_vma=False,
    )
```

time: 51.3 us -> 46.7 us (0.910)
  Pallas kernels: 26.1 us -> 21.2 us
    pallas_call x1, Pallas kernels: 10.2 us -> 7.23 us  [on_device(): pl.pallas_call(sweep_kernel, in_specs=[VMEM] * 7, out_specs=[ANY] + [VMEM...]
    pallas_call x1, Pallas kernels: 8 us -> 5.13 us  [on_device(): pl.pallas_call(stream_kernel, in_specs=[VMEM, VMEM, ANY], out_specs=[VMEM...]
    ppermute x3, waiting for transfers between devices: 2.79 us -> 1.01 us  [exchange(): lax.ppermute(even, 'wall', pairs(count, by, 0))]
    ppermute x3, waiting for transfers between devices: 2.04 us -> 3.82 us  [exchange(): lax.ppermute(odd, 'wall', pairs(count, by, 1))]
    pallas_call x2, Pallas kernels: 7.85 us -> 8.8 us  [the longest x1 4.68 us: on_device(): pl.pallas_call(edges_kernel, in_specs=[ANY, ANY], out_specs=[VMEM] * 7 +...]
  transfers between devices with their start and end apart: 7 -> 7, of which waited for: 2 -> 2; matrix products, arithmetic and copies ran while one was open for 0% -> 0% of each run, Pallas kernels for 16% -> 11%
where the time goes in v1:
time: 46.7 us; the launch traced here: 46.6 us
  Pallas kernels  21.2 us (45%)
  starting transfers between devices  18.8 us (40%)
  waiting for transfers between devices  4.84 us (10%)
  between operations  1.57 us (3%)
    ppermute x3, starting transfers between devices, exchange(): lax.ppermute(odd, 'wall', pairs(count, by, 1))  18.5 us
    pallas_call x1, Pallas kernels, on_device(): pl.pallas_call(sweep_kernel, in_specs=[VMEM] * 7, out_specs=[ANY] + [VMEM...  7.23 us
    pallas_call x1, Pallas kernels, on_device(): pl.pallas_call(stream_kernel, in_specs=[VMEM, VMEM, ANY], out_specs=[VMEM...  5.13 us
    pallas_call x1, Pallas kernels, on_device(): pl.pallas_call(edges_kernel, in_specs=[ANY, ANY], out_specs=[VMEM] * 7 +...  4.68 us
    pallas_call x1, Pallas kernels, on_device(): pl.pallas_call(finish_kernel, in_specs=[VMEM] * 8, out_specs=ANY, out_sha...  4.12 us
    ppermute x3, waiting for transfers between devices, exchange(): lax.ppermute(odd, 'wall', pairs(count, by, 1))  3.82 us
    ppermute x3, waiting for transfers between devices, exchange(): lax.ppermute(even, 'wall', pairs(count, by, 0))  1.01 us
  transfers between devices with their start and end apart: 7, of which 2 were waited for; matrix products, arithmetic and copies ran while one was open for 0% of the time, Pallas kernels for 11%

profile of v1, /device:TPU:96, one launch (start us, length us, event | category | flops | bytes accessed | tf_op | source)
XLA Modules:
  0.0 46.6 jit_solution(10850717639848884643)
XLA Ops:
  0.6 4.7 %edges.1 = (f32[10,24,8,8,128]{4,3,2,1,0:T(8,128)S(1)}, f32[2,10,24,8,128]{4,3,2,1,0:T(8,128)S(1)}, f32[2,2,10,8,128]{4,3,2,1,0:T(8,128)S(1)}, f32[2,10,8,128]{3...) custom-call(f32[10,24,8,8,1,128]{5,4,3,2,1,0:T(1,128)} %bitcast.22, ...), custom_call_target="tpu_custom_call" | custom-call | tf_op jit(solution)/shard_map/edges/pallas_call | solution.py:433
  5.3 0.1 collective-permute-start.2
  5.4 7.0 %collective-permute-start.3 = (f32[2,10,8,128]{3,2,1,0:T(8,128)S(1)}, f32[2,10,8,128]{3,2,1,0:T(8,128)S(1)}, u32[]{:S(2)}, u32[]{:S(2)}) collective-permute-start(f32[2,10,8,128]{3,2,1,0:T(8,128)S(1)} %get-tuple-element.99), channel_id=1, source_target_pairs={{2,4},{4,2},{6,8},{8,6},{10,12},{12,10},{14,16},{16,14},{18,20},{2... | collective-permute-start | bytes 245768 | tf_op jit(solution)/shard_map/ppermute | solution.py:379
  12.4 0.1 collective-permute-start.4
  12.5 0.0 collective-permute-done.2.sides
  12.5 5.1 %streamwise.1 = (f32[10,24,8,8,128]{4,3,2,1,0:T(8,128)S(1)}, f32[2,24,8,8,128]{4,3,2,1,0:T(8,128)S(1)}) custom-call(f32[10,24,8,8,128]{4,3,2,1,0:T(8,128)S(1)} %get-tuple-element.94.field, f32[2,10,24,8,128]{4,3,2,1,0:T(8,128)S(1)} %collective-permute-done.2.sides, f32[2,24,8,8,1,128]{5,4,3,2,1,0:T(1,128)} %bitcast.24), custom_call_target="tpu_custom_call" | custom-call | flops 4000000000 | tf_op jit(solution)/shard_map/streamwise/pallas_call | solution.py:454
  17.6 0.0 collective-permute-done.3.odd_in
  17.6 0.0 collective-permute-done.4.even_in
  17.6 7.2 %sweeps.1 = (f32[10,24,8,8,1,128]{5,4,3,2,1,0:T(1,128)}, f32[10,24,8,8,128]{4,3,2,1,0:T(8,128)S(1)}, f32[2,10,8,128]{3,2,1,0:T(8,128)S(1)}, f32[10,8,128]{2,1,0:...) custom-call(f32[5,6,8,128]{3,2,1,0:T(8,128)S(1)} %get-tuple-element.93.coef, ...), custom_call_target="tpu_custom_call" | custom-call | tf_op jit(solution)/shard_map/sweeps/pallas_call | solution.py:465
  24.9 5.7 %collective-permute-start.5 = (f32[10,8,128]{2,1,0:T(8,128)S(1)}, f32[10,8,128]{2,1,0:T(8,128)S(1)}, u32[]{:S(2)}, u32[]{:S(2)}) collective-permute-start(f32[10,8,128]{2,1,0:T(8,128)S(1)} %get-tuple-element.106), channel_id=1, source_target_pairs={{2,4},{4,2},{6,8},{8,6},{10,12},{12,10},{14,16},{16,14},{18,20},{2... | collective-permute-start | bytes 122888 | tf_op jit(solution)/shard_map/ppermute | solution.py:379
  30.6 0.1 collective-permute-start.6
  30.6 5.8 %collective-permute-start.7 = (f32[10,8,128]{2,1,0:T(8,128)S(1)}, f32[10,8,128]{2,1,0:T(8,128)S(1)}, u32[]{:S(2)}, u32[]{:S(2)}) collective-permute-start(f32[10,8,128]{2,1,0:T(8,128)S(1)} %get-tuple-element.108), channel_id=1, source_target_pairs={{4,8},{8,4},{6,10},{10,6},{12,16},{16,12},{14,18},{18,14},{20,24},... | collective-permute-start | bytes 122888 | tf_op jit(solution)/shard_map/ppermute | solution.py:379
  36.5 0.1 collective-permute-start.8
  37.2 0.0 collective-permute-done.5.odd1
  37.2 0.0 collective-permute-done.6.even1
  37.2 3.8 %collective-permute-done.7.odd2 = f32[10,8,128]{2,1,0:T(8,128)S(1)} collective-permute-done((f32[10,8,128]{2,1,0:T(8,128)S(1)}, f32[10,8,128]{2,1,0:T(8,128)S(1)}, u32[]{:S(2)}, u32[]{:S(2)}) %collective-permute-start.7) | collective-permute-done | bytes 40992 | tf_op jit(solution)/shard_map/ppermute | solution.py:379
  41.1 1.0 %collective-permute-done.8.even2 = f32[10,8,128]{2,1,0:T(8,128)S(1)} collective-permute-done((f32[10,8,128]{2,1,0:T(8,128)S(1)}, f32[10,8,128]{2,1,0:T(8,128)S(1)}, u32[]{:S(2)}, u32[]{:S(2)}) %collective-permute-start.8) | collective-permute-done | bytes 40992 | tf_op jit(solution)/shard_map/ppermute | solution.py:380
  42.1 4.1 %finish.1 = f32[10,24,8,8,1,128]{5,4,3,2,1,0:T(1,128)} custom-call(f32[5,6,8,128]{3,2,1,0:T(8,128)S(1)} %get-tuple-element.93.coef, f32[5,24,8,128]{3,2,1,0:T(8,128)S(1)} %get-tuple-element.103.fading, f32[10,24,8,8,128]{4,3,2,1,0:T(8,128)S(1)} %get-tuple-element.104.partial, f32[2,10,8,128]{3,2,1,0:T(8,128)S(1)} %get-tuple-element.105.total, ...), custom_call_target="tpu_custom_call" | custom-call | tf_op jit(solution)/shard_map/finish/pallas_call | solution.py:480
  46.2 0.2 conditional.1
Async XLA Ops:
  5.3 7.2 %collective-permute-start.2 = (f32[2,10,24,8,128]{4,3,2,1,0:T(8,128)S(1)}, f32[2,10,24,8,128]{4,3,2,1,0:T(8,128)S(1)}, u32[]{:S(2)}, u32[]{:S(2)}) collective-permute-start(f32[2,10,24,8,128]{4,3,2,1,0:T(8,128)S(1)} %get-tuple-element.95), channel_id=1, source_target_pairs={{0,1},{1,0},{2,3},{3,2},{4,5},{5,4},{6,7},{7,6},{8,9},{9,8},{10,11... | collective-permute-start | bytes 5898248 | tf_op jit(solution)/shard_map/ppermute | solution.py:451
  5.4 12.2 %collective-permute-start.3 = (f32[2,10,8,128]{3,2,1,0:T(8,128)S(1)}, f32[2,10,8,128]{3,2,1,0:T(8,128)S(1)}, u32[]{:S(2)}, u32[]{:S(2)}) collective-permute-start(f32[2,10,8,128]{3,2,1,0:T(8,128)S(1)} %get-tuple-element.99), channel_id=1, source_target_pairs={{2,4},{4,2},{6,8},{8,6},{10,12},{12,10},{14,16},{16,14},{18,20},{2... | collective-permute-start | bytes 245768 | tf_op jit(solution)/shard_map/ppermute | solution.py:379
  12.4 5.3 %collective-permute-start.4 = (f32[2,10,8,128]{3,2,1,0:T(8,128)S(1)}, f32[2,10,8,128]{3,2,1,0:T(8,128)S(1)}, u32[]{:S(2)}, u32[]{:S(2)}) collective-permute-start(f32[2,10,8,128]{3,2,1,0:T(8,128)S(1)} %get-tuple-element.100), channel_id=1, source_target_pairs={{0,2},{2,0},{4,6},{6,4},{8,10},{10,8},{12,14},{14,12},{16,18},{18,... | collective-permute-start | bytes 245768 | tf_op jit(solution)/shard_map/ppermute | solution.py:380
  24.9 12.4 %collective-permute-start.5 = (f32[10,8,128]{2,1,0:T(8,128)S(1)}, f32[10,8,128]{2,1,0:T(8,128)S(1)}, u32[]{:S(2)}, u32[]{:S(2)}) collective-permute-start(f32[10,8,128]{2,1,0:T(8,128)S(1)} %get-tuple-element.106), channel_id=1, source_target_pairs={{2,4},{4,2},{6,8},{8,6},{10,12},{12,10},{14,16},{16,14},{18,20},{2... | collective-permute-start | bytes 122888 | tf_op jit(solution)/shard_map/ppermute | solution.py:379
  30.6 6.7 %collective-permute-start.6 = (f32[10,8,128]{2,1,0:T(8,128)S(1)}, f32[10,8,128]{2,1,0:T(8,128)S(1)}, u32[]{:S(2)}, u32[]{:S(2)}) collective-permute-start(f32[10,8,128]{2,1,0:T(8,128)S(1)} %get-tuple-element.107), channel_id=1, source_target_pairs={{0,2},{2,0},{4,6},{6,4},{8,10},{10,8},{12,14},{14,12},{16,18},{18,... | collective-permute-start | bytes 122888 | tf_op jit(solution)/shard_map/ppermute | solution.py:380
  30.6 10.4 %collective-permute-start.7 = (f32[10,8,128]{2,1,0:T(8,128)S(1)}, f32[10,8,128]{2,1,0:T(8,128)S(1)}, u32[]{:S(2)}, u32[]{:S(2)}) collective-permute-start(f32[10,8,128]{2,1,0:T(8,128)S(1)} %get-tuple-element.108), channel_id=1, source_target_pairs={{4,8},{8,4},{6,10},{10,6},{12,16},{16,12},{14,18},{18,14},{20,24},... | collective-permute-start | bytes 122888 | tf_op jit(solution)/shard_map/ppermute | solution.py:379
  36.5 5.6 %collective-permute-start.8 = (f32[10,8,128]{2,1,0:T(8,128)S(1)}, f32[10,8,128]{2,1,0:T(8,128)S(1)}, u32[]{:S(2)}, u32[]{:S(2)}) collective-permute-start(f32[10,8,128]{2,1,0:T(8,128)S(1)} %get-tuple-element.109), channel_id=1, source_target_pairs={{0,4},{4,0},{2,6},{6,2},{8,12},{12,8},{10,14},{14,10},{16,20},{20,... | collective-permute-start | bytes 122888 | tf_op jit(solution)/shard_map/ppermute | solution.py:380

commit v2 on v1

--- a/solution.py
+++ b/solution.py
@@ -21,6 +21,7 @@
 slope_edge = -mix / slope_gain
 tiny = 1.1754943508222875e-38
 SPLIT = 6
+TOGETHER = 2
 f32 = jnp.float32
 MIB = 1 << 20
 
@@ -146,30 +147,32 @@
         low = (x - high.astype(f32)).astype(jnp.bfloat16)
         return jnp.dot(jnp.concatenate([high, low], axis=1), columns, preferred_element_type=f32)
 
-    before = spread(sides[1].reshape(planes * tiles * 8, 128), matrix[:, 128:])
-    after = spread(sides[0].reshape(planes * tiles * 8, 128), matrix[:, 128:])
+    outside = spread(sides[...].reshape(2 * planes * tiles * 8, 128), matrix[:, 128:])
+    after, before = outside[: planes * tiles * 8], outside[planes * tiles * 8 :]
     first = lax.broadcasted_iota(jnp.int32, before.shape, 1) < 64
     near[...] = jnp.where(first, before, after).reshape(planes, tiles, 8, 128)
 
-    def body(p, carry):
-        both = spread(field[p].reshape(tiles * 64, 128), matrix)
-        for tile in range(tiles):
-            for r in range(8):
-                at = tile * 64 + 8 * r
-                part = both[at : at + 8, 128:]
-                part = jnp.where(left, pltpu.roll(part, 1, 0), pltpu.roll(part, 7, 0))
-                part = jnp.where(outer, jnp.broadcast_to(near[p, tile, r : r + 1, :], (8, 128)), part)
-                speed = field[p % 2, tile, r] * (-1.0 / 60.0)
-                out[p, tile, r] = speed * (both[at : at + 8, :128] + part)
+    def body(g, carry):
+        both = spread(field[pl.ds(g * TOGETHER, TOGETHER)].reshape(TOGETHER * tiles * 64, 128), matrix)
+        for q in range(TOGETHER):
+            p = g * TOGETHER + q
+            for tile in range(tiles):
+                for r in range(8):
+                    at = (q * tiles + tile) * 64 + 8 * r
+                    part = both[at : at + 8, 128:]
+                    part = jnp.where(left, pltpu.roll(part, 1, 0), pltpu.roll(part, 7, 0))
+                    part = jnp.where(outer, jnp.broadcast_to(near[p, tile, r : r + 1, :], (8, 128)), part)
+                    speed = field[q % 2, tile, r] * (-1.0 / 60.0)
+                    out[p, tile, r] = speed * (both[at : at + 8, :128] + part)
         return carry
 
-    lax.fori_loop(0, planes, body, 0)
+    lax.fori_loop(0, planes // TOGETHER, body, 0)
     for copy in copies:
         copy.wait()
 
 
 def sweep_kernel(
-    coef, field, stream, wall, own, odd_in, even_in, tend_hbm, adv, total, odd1, even1, odd2, even2, work, tend, sems
+    coef, fading, field, stream, wall, own, odd_in, even_in, tend, work, total, odd1, even1, odd2, even2
 ):
     planes, tiles = field.shape[0], field.shape[1]
     count = planes // 2
@@ -191,7 +194,6 @@
 
     every = range(planes)
     ratio = [coef[k, 0] for k in ks]
-    copies = []
     zero = jnp.zeros((8, 128), f32)
 
     def rise(t, u):
@@ -203,13 +205,13 @@
 
     lax.fori_loop(0, tiles, rise, [below(0, p) for p in every])
 
-    bottom = {}
+    top, bottom = {}, {}
     for z in range(2):
         at = [2 * k + z for k in ks]
         ghost = [below(1, at[k]) for k in ks]
 
         def fall(i, carry, z=z, at=at, ghost=ghost):
-            v, ahead, here, total = carry
+            v, ahead, here, total, upper = carry
             t = tiles - 1 - i
             for r in range(7, -1, -1):
                 speed = wall[z, t, r] * (-slope_gain)
@@ -224,39 +226,30 @@
                 rate = [stream[at[k], t, r] + speed * slope[k] for k in ks]
                 for k in ks:
                     tend[at[k], t, r] = rate[k]
-                total = [(rate[k] + 8.0 * here[k]) + ratio[k] * total[k] for k in ks]
+                source = [rate[k] + 8.0 * here[k] for k in ks]
+                grow = [jnp.broadcast_to(fading[k, i, 7 - r : 8 - r, :], (8, 128)) for k in ks]
+                upper = [upper[k] + grow[k] * source[k] for k in ks]
+                total = [source[k] + ratio[k] * total[k] for k in ks]
                 for k in ks:
                     work[at[k], t, r] = total[k]
                 v = [here[k] + slope_ratio * v[k] for k in ks]
                 ahead, here = here, last
-            return v, ahead, here, total
+            return v, ahead, here, total, upper
 
         start = (
             [above(0, at[k]) for k in ks],
             [above(1, at[k]) for k in ks],
             [field[at[k], tiles - 1, 7] for k in ks],
             [zero] * count,
+            [zero] * count,
         )
-        lowest = lax.fori_loop(0, tiles, fall, start)[3]
+        lowest, upper = lax.fori_loop(0, tiles, fall, start)[3:]
         for k in ks:
             bottom[at[k]] = lowest[k]
-            for copy in store_rows(tend, tend_hbm, sems, at[k]):
-                copy.start()
-                copies.append(copy)
-    gain = [coef[k, 1] for k in ks]
-
-    def settle(t, q):
-        for r in range(8):
-            q = [work[p, t, r] + ratio[p // 2] * q[p] for p in every]
-            for p in every:
-                adv[p, t, r] = gain[p // 2] * q[p] - field[p, t, r]
-        return q
-
-    top = lax.fori_loop(0, tiles, settle, [zero] * planes)
+            top[at[k]] = upper[k] / ratio[k]
     for p in every:
         weight, step = coef[p // 2, 3], ratio[p // 2]
-        up = coef[p // 2, 2] * top[p] + weight * step * bottom[p]
-        down = bottom[p]
+        up, down = top[p], bottom[p]
         total[0, p] = up
         total[1, p] = down
         send_up = jnp.where(first, up - weight * step * down, up)
@@ -265,6 +258,25 @@
         even1[p] = jnp.where(odd, send_down, send_up)
         odd2[p] = jnp.where(pair, send_up, send_down)
         even2[p] = jnp.where(pair, send_down, send_up)
+
+
+def settle_kernel(coef, field, work, tend, tend_hbm, adv, sems):
+    planes, tiles = field.shape[0], field.shape[1]
+    every = range(planes)
+    copies = sum([store_rows(tend, tend_hbm, sems, p) for p in every], [])
+    for copy in copies:
+        copy.start()
+    ratio = [coef[k, 0] for k in range(planes // 2)]
+    gain = [coef[k, 1] for k in range(planes // 2)]
+
+    def settle(t, q):
+        for r in range(8):
+            q = [work[p, t, r] + ratio[p // 2] * q[p] for p in every]
+            for p in every:
+                adv[p, t, r] = gain[p // 2] * q[p] - field[p, t, r]
+        return q
+
+    lax.fori_loop(0, tiles, settle, [jnp.zeros((8, 128), f32)] * planes)
     for copy in copies:
         copy.wait()
 
@@ -462,20 +474,30 @@
         name="streamwise",
     )(field, sides, in_hbm(wall_source))
 
-    tendency, partial, total, *sent = pl.pallas_call(
+    rate, work, total, *sent = pl.pallas_call(
         sweep_kernel,
-        in_specs=[VMEM] * 7,
-        out_specs=[ANY] + [VMEM] * 6,
-        out_shape=[shape(source.shape, f32), resident, pltpu.VMEM((2, planes, 8, 128), f32)] + [rows] * 4,
-        scratch_shapes=[pltpu.VMEM(full, f32), pltpu.VMEM(full, f32), plane_sems],
-        compiler_params=params(18),
+        in_specs=[VMEM] * 8,
+        out_specs=[VMEM] * 7,
+        out_shape=[resident, resident, pltpu.VMEM((2, planes, 8, 128), f32)] + [rows] * 4,
+        compiler_params=params(2),
         name="sweeps",
-    )(coef, field, stream, wall, own, odd, even)
+    )(coef, fading, field, stream, wall, own, odd, even)
 
     odd1, even1, odd2, even2 = sent
     far = exchange(odd2, even2, 2)
     near = exchange(odd1, even1, 1)
     arrived = [*near, *far]
+
+    tendency, partial = pl.pallas_call(
+        settle_kernel,
+        in_specs=[VMEM] * 4,
+        out_specs=[ANY, VMEM],
+        out_shape=[shape(source.shape, f32), resident],
+        scratch_shapes=[plane_sems],
+        compiler_params=params(2),
+        cost_estimate=pl.CostEstimate(flops=4_000_000_000, transcendentals=0, bytes_accessed=0),
+        name="settle",
+    )(coef, field, work, rate)
 
     advanced = pl.pallas_call(
         finish_kernel,

time: 46.7 us -> 44.5 us (0.953)
  waiting for transfers between devices: 4.84 us -> 1.67 us
  Pallas kernels: 21.2 us -> 22.1 us
    ppermute x3, waiting for transfers between devices: 3.82 us -> 0.72 us  [exchange(): lax.ppermute(odd, 'wall', pairs(count, by, 1))]
    pallas_call x1 -> x2, Pallas kernels: 7.23 us -> 8.9 us  [the longest x1 5.1 us: on_device(): pl.pallas_call(sweep_kernel, in_specs=[VMEM] * 8, out_specs=[VMEM] * 7, o...]
    pallas_call x1, Pallas kernels: 5.13 us -> 4.42 us  [on_device(): pl.pallas_call(stream_kernel, in_specs=[VMEM, VMEM, ANY], out_specs=[VMEM...]
  transfers between devices with their start and end apart: 7 -> 7, of which waited for: 2 -> 2; matrix products, arithmetic and copies ran while one was open for 0% -> 0% of each run, Pallas kernels for 11% -> 19%
where the time goes in v2:
time: 44.5 us; the launch traced here: 44.4 us
  Pallas kernels  22.1 us (50%)
  starting transfers between devices  18.8 us (42%)
  waiting for transfers between devices  1.67 us (4%)
  between operations  1.57 us (4%)
    ppermute x3, starting transfers between devices, exchange(): lax.ppermute(odd, 'wall', pairs(count, by, 1))  18.5 us
    pallas_call x1, Pallas kernels, on_device(): pl.pallas_call(sweep_kernel, in_specs=[VMEM] * 8, out_specs=[VMEM] * 7, o...  5.1 us
    pallas_call x1, Pallas kernels, on_device(): pl.pallas_call(edges_kernel, in_specs=[ANY, ANY], out_specs=[VMEM] * 7 +...  4.68 us
    pallas_call x1, Pallas kernels, on_device(): pl.pallas_call(stream_kernel, in_specs=[VMEM, VMEM, ANY], out_specs=[VMEM...  4.42 us
    pallas_call x1, Pallas kernels, on_device(): pl.pallas_call(finish_kernel, in_specs=[VMEM] * 8, out_specs=ANY, out_sha...  4.12 us
    pallas_call x1, Pallas kernels, on_device(): pl.pallas_call(settle_kernel, in_specs=[VMEM] * 4, out_specs=[ANY, VMEM],...  3.8 us
    ppermute x3, waiting for transfers between devices, exchange(): lax.ppermute(even, 'wall', pairs(count, by, 0))  0.95 us
  transfers between devices with their start and end apart: 7, of which 2 were waited for; matrix products, arithmetic and copies ran while one was open for 0% of the time, Pallas kernels for 19%

profile of v2, /device:TPU:96, one launch (start us, length us, event | category | flops | bytes accessed | tf_op | source)
XLA Modules:
  0.0 44.4 jit_solution(10030633780744700142)
XLA Ops:
  0.6 4.7 %edges.1 = (f32[10,24,8,8,128]{4,3,2,1,0:T(8,128)S(1)}, f32[2,10,24,8,128]{4,3,2,1,0:T(8,128)S(1)}, f32[2,2,10,8,128]{4,3,2,1,0:T(8,128)S(1)}, f32[2,10,8,128]{3...) custom-call(f32[10,24,8,8,1,128]{5,4,3,2,1,0:T(1,128)} %bitcast.22, ...), custom_call_target="tpu_custom_call" | custom-call | tf_op jit(solution)/shard_map/edges/pallas_call | solution.py:445
  5.3 0.1 collective-permute-start.2
  5.4 7.0 %collective-permute-start.3 = (f32[2,10,8,128]{3,2,1,0:T(8,128)S(1)}, f32[2,10,8,128]{3,2,1,0:T(8,128)S(1)}, u32[]{:S(2)}, u32[]{:S(2)}) collective-permute-start(f32[2,10,8,128]{3,2,1,0:T(8,128)S(1)} %get-tuple-element.102), channel_id=1, source_target_pairs={{2,4},{4,2},{6,8},{8,6},{10,12},{12,10},{14,16},{16,14},{18,20},{2... | collective-permute-start | bytes 245768 | tf_op jit(solution)/shard_map/ppermute | solution.py:391
  12.4 0.1 collective-permute-start.4
  13.1 0.0 collective-permute-done.2.sides
  13.1 4.4 %streamwise.1 = (f32[10,24,8,8,128]{4,3,2,1,0:T(8,128)S(1)}, f32[2,24,8,8,128]{4,3,2,1,0:T(8,128)S(1)}) custom-call(f32[10,24,8,8,128]{4,3,2,1,0:T(8,128)S(1)} %get-tuple-element.96.field, f32[2,10,24,8,128]{4,3,2,1,0:T(8,128)S(1)} %collective-permute-done.2.sides, f32[2,24,8,8,1,128]{5,4,3,2,1,0:T(1,128)} %bitcast.24), custom_call_target="tpu_custom_call" | custom-call | flops 4000000000 | tf_op jit(solution)/shard_map/streamwise/pallas_call | solution.py:466
  17.5 0.0 collective-permute-done.3.odd_in
  17.6 0.0 collective-permute-done.4.even_in
  17.6 5.1 %sweeps.1 = (f32[10,24,8,8,128]{4,3,2,1,0:T(8,128)S(1)}, f32[10,24,8,8,128]{4,3,2,1,0:T(8,128)S(1)}, f32[2,10,8,128]{3,2,1,0:T(8,128)S(1)}, f32[10,8,128]{2,1,0:...) custom-call(f32[5,6,8,128]{3,2,1,0:T(8,128)S(1)} %get-tuple-element.95.coef, ...), custom_call_target="tpu_custom_call" | custom-call | tf_op jit(solution)/shard_map/sweeps/pallas_call | solution.py:477
  22.7 5.7 %collective-permute-start.5 = (f32[10,8,128]{2,1,0:T(8,128)S(1)}, f32[10,8,128]{2,1,0:T(8,128)S(1)}, u32[]{:S(2)}, u32[]{:S(2)}) collective-permute-start(f32[10,8,128]{2,1,0:T(8,128)S(1)} %get-tuple-element.110), channel_id=1, source_target_pairs={{2,4},{4,2},{6,8},{8,6},{10,12},{12,10},{14,16},{16,14},{18,20},{2... | collective-permute-start | bytes 122888 | tf_op jit(solution)/shard_map/ppermute | solution.py:391
  28.4 0.1 collective-permute-start.6
  28.5 5.8 %collective-permute-start.7 = (f32[10,8,128]{2,1,0:T(8,128)S(1)}, f32[10,8,128]{2,1,0:T(8,128)S(1)}, u32[]{:S(2)}, u32[]{:S(2)}) collective-permute-start(f32[10,8,128]{2,1,0:T(8,128)S(1)} %get-tuple-element.112), channel_id=1, source_target_pairs={{4,8},{8,4},{6,10},{10,6},{12,16},{16,12},{14,18},{18,14},{20,24},... | collective-permute-start | bytes 122888 | tf_op jit(solution)/shard_map/ppermute | solution.py:391
  34.3 0.1 collective-permute-start.8
  34.4 3.8 %settle.1 = (f32[10,24,8,8,1,128]{5,4,3,2,1,0:T(1,128)}, f32[10,24,8,8,128]{4,3,2,1,0:T(8,128)S(1)}) custom-call(f32[5,6,8,128]{3,2,1,0:T(8,128)S(1)} %get-tuple-element.95.coef, f32[10,24,8,8,128]{4,3,2,1,0:T(8,128)S(1)} %get-tuple-element.96.field, f32[10,24,8,8,128]{4,3,2,1,0:T(8,128)S(1)} %get-tuple-element.104.work, ...), custom_call_target="tpu_custom_call" | custom-call | flops 4000000000 | tf_op jit(solution)/shard_map/settle/pallas_call | solution.py:491
  38.2 0.0 collective-permute-done.5.odd1
  38.2 0.0 collective-permute-done.6.even1
  38.2 0.7 %collective-permute-done.7.odd2 = f32[10,8,128]{2,1,0:T(8,128)S(1)} collective-permute-done((f32[10,8,128]{2,1,0:T(8,128)S(1)}, f32[10,8,128]{2,1,0:T(8,128)S(1)}, u32[]{:S(2)}, u32[]{:S(2)}) %collective-permute-start.7) | collective-permute-done | bytes 40992 | tf_op jit(solution)/shard_map/ppermute | solution.py:391
  38.9 0.9 %collective-permute-done.8.even2 = f32[10,8,128]{2,1,0:T(8,128)S(1)} collective-permute-done((f32[10,8,128]{2,1,0:T(8,128)S(1)}, f32[10,8,128]{2,1,0:T(8,128)S(1)}, u32[]{:S(2)}, u32[]{:S(2)}) %collective-permute-start.8) | collective-permute-done | bytes 40992 | tf_op jit(solution)/shard_map/ppermute | solution.py:392
  39.9 4.1 %finish.1 = f32[10,24,8,8,1,128]{5,4,3,2,1,0:T(1,128)} custom-call(f32[5,6,8,128]{3,2,1,0:T(8,128)S(1)} %get-tuple-element.95.coef, f32[5,24,8,128]{3,2,1,0:T(8,128)S(1)} %get-tuple-element.97.fading, f32[10,24,8,8,128]{4,3,2,1,0:T(8,128)S(1)} %get-tuple-element.108.partial, f32[2,10,8,128]{3,2,1,0:T(8,128)S(1)} %get-tuple-element.109.total, ...), custom_call_target="tpu_custom_call" | custom-call | tf_op jit(solution)/shard_map/finish/pallas_call | solution.py:502
  44.0 0.2 conditional.1
Async XLA Ops:
  5.3 7.8 %collective-permute-start.2 = (f32[2,10,24,8,128]{4,3,2,1,0:T(8,128)S(1)}, f32[2,10,24,8,128]{4,3,2,1,0:T(8,128)S(1)}, u32[]{:S(2)}, u32[]{:S(2)}) collective-permute-start(f32[2,10,24,8,128]{4,3,2,1,0:T(8,128)S(1)} %get-tuple-element.98), channel_id=1, source_target_pairs={{0,1},{1,0},{2,3},{3,2},{4,5},{5,4},{6,7},{7,6},{8,9},{9,8},{10,11... | collective-permute-start | bytes 5898248 | tf_op jit(solution)/shard_map/ppermute | solution.py:463
  5.4 12.1 %collective-permute-start.3 = (f32[2,10,8,128]{3,2,1,0:T(8,128)S(1)}, f32[2,10,8,128]{3,2,1,0:T(8,128)S(1)}, u32[]{:S(2)}, u32[]{:S(2)}) collective-permute-start(f32[2,10,8,128]{3,2,1,0:T(8,128)S(1)} %get-tuple-element.102), channel_id=1, source_target_pairs={{2,4},{4,2},{6,8},{8,6},{10,12},{12,10},{14,16},{16,14},{18,20},{2... | collective-permute-start | bytes 245768 | tf_op jit(solution)/shard_map/ppermute | solution.py:391
  12.4 5.2 %collective-permute-start.4 = (f32[2,10,8,128]{3,2,1,0:T(8,128)S(1)}, f32[2,10,8,128]{3,2,1,0:T(8,128)S(1)}, u32[]{:S(2)}, u32[]{:S(2)}) collective-permute-start(f32[2,10,8,128]{3,2,1,0:T(8,128)S(1)} %get-tuple-element.103), channel_id=1, source_target_pairs={{0,2},{2,0},{4,6},{6,4},{8,10},{10,8},{12,14},{14,12},{16,18},{18,... | collective-permute-start | bytes 245768 | tf_op jit(solution)/shard_map/ppermute | solution.py:392
  22.7 15.5 %collective-permute-start.5 = (f32[10,8,128]{2,1,0:T(8,128)S(1)}, f32[10,8,128]{2,1,0:T(8,128)S(1)}, u32[]{:S(2)}, u32[]{:S(2)}) collective-permute-start(f32[10,8,128]{2,1,0:T(8,128)S(1)} %get-tuple-element.110), channel_id=1, source_target_pairs={{2,4},{4,2},{6,8},{8,6},{10,12},{12,10},{14,16},{16,14},{18,20},{2... | collective-permute-start | bytes 122888 | tf_op jit(solution)/shard_map/ppermute | solution.py:391
  28.4 9.8 %collective-permute-start.6 = (f32[10,8,128]{2,1,0:T(8,128)S(1)}, f32[10,8,128]{2,1,0:T(8,128)S(1)}, u32[]{:S(2)}, u32[]{:S(2)}) collective-permute-start(f32[10,8,128]{2,1,0:T(8,128)S(1)} %get-tuple-element.111), channel_id=1, source_target_pairs={{0,2},{2,0},{4,6},{6,4},{8,10},{10,8},{12,14},{14,12},{16,18},{18,... | collective-permute-start | bytes 122888 | tf_op jit(solution)/shard_map/ppermute | solution.py:392
  28.5 10.4 %collective-permute-start.7 = (f32[10,8,128]{2,1,0:T(8,128)S(1)}, f32[10,8,128]{2,1,0:T(8,128)S(1)}, u32[]{:S(2)}, u32[]{:S(2)}) collective-permute-start(f32[10,8,128]{2,1,0:T(8,128)S(1)} %get-tuple-element.112), channel_id=1, source_target_pairs={{4,8},{8,4},{6,10},{10,6},{12,16},{16,12},{14,18},{18,14},{20,24},... | collective-permute-start | bytes 122888 | tf_op jit(solution)/shard_map/ppermute | solution.py:391
  34.3 5.6 %collective-permute-start.8 = (f32[10,8,128]{2,1,0:T(8,128)S(1)}, f32[10,8,128]{2,1,0:T(8,128)S(1)}, u32[]{:S(2)}, u32[]{:S(2)}) collective-permute-start(f32[10,8,128]{2,1,0:T(8,128)S(1)} %get-tuple-element.113), channel_id=1, source_target_pairs={{0,4},{4,0},{2,6},{6,2},{8,12},{12,8},{10,14},{14,10},{16,20},{20,... | collective-permute-start | bytes 122888 | tf_op jit(solution)/shard_map/ppermute | solution.py:392

commit v3 on v2

--- a/solution.py
+++ b/solution.py
@@ -55,6 +55,10 @@
 def place():
     here = lax.axis_index("wall")
     return here, here == 0, here == lax.axis_size("wall") - 1
+
+
+def carries_near():
+    return lax.axis_index("stream") == 0
 
 
 def edges_kernel(field_hbm, diffusion_hbm, field, sides, own, odd_out, even_out, coef, fading, flag, rate, sems, sem):
@@ -172,7 +176,7 @@
 
 
 def sweep_kernel(
-    coef, fading, field, stream, wall, own, odd_in, even_in, tend, work, total, odd1, even1, odd2, even2
+    coef, fading, field, stream, wall, own, odd_in, even_in, tend, work, total, keep, give
 ):
     planes, tiles = field.shape[0], field.shape[1]
     count = planes // 2
@@ -254,10 +258,17 @@
         total[1, p] = down
         send_up = jnp.where(first, up - weight * step * down, up)
         send_down = jnp.where(last_block, down - weight * step * up, down)
-        odd1[p] = jnp.where(odd, send_up, send_down)
-        even1[p] = jnp.where(odd, send_down, send_up)
-        odd2[p] = jnp.where(pair, send_up, send_down)
-        even2[p] = jnp.where(pair, send_down, send_up)
+        near = jnp.where(odd, send_up, send_down), jnp.where(odd, send_down, send_up)
+        far = jnp.where(pair, send_up, send_down), jnp.where(pair, send_down, send_up)
+        for i in range(2):
+            keep[i, p] = jnp.where(carries_near(), near[i], far[i])
+            give[i, p] = jnp.where(carries_near(), far[i], near[i])
+
+
+def pack_kernel(keep, got, odd, even):
+    for i, target in enumerate((odd, even)):
+        target[0] = keep[i]
+        target[1] = got[i]
 
 
 def settle_kernel(coef, field, work, tend, tend_hbm, adv, sems):
@@ -281,13 +292,16 @@
         copy.wait()
 
 
-def two_blocks(p, coef, total, odd1, even1, odd2, even2):
+def two_blocks(p, coef, total, odd_own, even_own, odd_other, even_other):
     here, first, last_block = place()
     odd = here % 2 == 1
     pair = (here // 2) % 2 == 1
+    mine, other = (odd_own[0, p], even_own[0, p]), (odd_other[1, p], even_other[1, p])
+    odd1, even1 = [jnp.where(carries_near(), a, b) for a, b in zip(mine, other)]
+    odd2, even2 = [jnp.where(carries_near(), b, a) for a, b in zip(mine, other)]
     ratio, weight = coef[p // 2, 0], coef[p // 2, 3]
-    low = jnp.where(odd, even1[p], odd1[p]) + weight * jnp.where(pair, even2[p], odd2[p])
-    high = jnp.where(odd, odd1[p], even1[p]) + weight * jnp.where(pair, odd2[p], even2[p])
+    low = jnp.where(odd, even1, odd1) + weight * jnp.where(pair, even2, odd2)
+    high = jnp.where(odd, odd1, even1) + weight * jnp.where(pair, odd2, even2)
     end_low = -ratio * (total[1, p] + weight * high)
     end_high = -ratio * (total[0, p] + weight * low)
     return jnp.where(first, end_low, low), jnp.where(last_block, end_high, high)
@@ -307,13 +321,13 @@
     lax.fori_loop(0, tiles, body, 0)
 
 
-def finish_kernel(coef, fading, partial, total, odd1, even1, odd2, even2, out_hbm, out, sems):
+def finish_kernel(coef, fading, partial, total, odd_own, even_own, odd_other, even_other, out_hbm, out, sems):
     copies = []
     for k in range(coef.shape[0]):
         ratio, scale = coef[k, 0], coef[k, 5]
         lows, highs = [], []
         for p in (2 * k, 2 * k + 1):
-            low, high = two_blocks(p, coef, total, odd1, even1, odd2, even2)
+            low, high = two_blocks(p, coef, total, odd_own, even_own, odd_other, even_other)
             lows.append(scale * (ratio * total[1, p] + low))
             highs.append(scale * high)
         add_ends(k, lows, highs, fading, partial, out)
@@ -344,14 +358,28 @@
 
 
 def chain_end_kernel(
-    advanced_hbm, coef, fading, total, odd1, even1, odd2, even2, low, high, out_hbm, before, after, loads, stores
+    advanced_hbm,
+    coef,
+    fading,
+    total,
+    odd_own,
+    even_own,
+    odd_other,
+    even_other,
+    low,
+    high,
+    out_hbm,
+    before,
+    after,
+    loads,
+    stores,
 ):
     for k in range(coef.shape[0]):
         pair = (2 * k, 2 * k + 1)
         scale = coef[k, 5]
         lows, highs = [], []
         for p in pair:
-            near_low, near_high = two_blocks(p, coef, total, odd1, even1, odd2, even2)
+            near_low, near_high = two_blocks(p, coef, total, odd_own, even_own, odd_other, even_other)
             lows.append(scale * (low[p] - near_low))
             highs.append(scale * (high[p] - near_high))
         copies = sum([load_rows(advanced_hbm, before, loads, p) for p in pair], [])
@@ -385,12 +413,14 @@
     return (planes, tiles, 8, 8, 128)
 
 
-def exchange(odd, even, by):
-    count = lax.axis_size("wall")
-    return (
-        lax.ppermute(odd, "wall", pairs(count, by, 1)),
-        lax.ppermute(even, "wall", pairs(count, by, 0)),
-    )
+def swap(x):
+    return lax.ppermute(x, "stream", [(0, 1), (1, 0)])
+
+
+def carried(x, odd):
+    count, cores = lax.axis_size("wall"), lax.axis_size("stream")
+    moves = [(cores * a + c, cores * b + c) for c in range(cores) for a, b in pairs(count, c + 1, odd)]
+    return lax.ppermute(x, ("wall", "stream"), moves)
 
 
 def whole_chain(advanced, coef, fading, total, *arrived):
@@ -437,7 +467,6 @@
     source, wall_source = lines(fields), lines(wall_velocity)
     full = row_shape(source.shape)
     resident = pltpu.VMEM(full, f32)
-    rows = shape((planes, 8, 128), f32)
     ends = shape((2, planes, 8, 128), f32)
     in_hbm = functools.partial(pltpu.with_memory_space_constraint, memory_space=pltpu.HBM)
     plane_sems = pltpu.SemaphoreType.DMA((planes, 8))
@@ -460,8 +489,10 @@
         compiler_params=params(4),
         name="edges",
     )(in_hbm(source), in_hbm(diffusion))
-    sides = lax.ppermute(sides, "stream", [(0, 1), (1, 0)])
-    odd, even = exchange(odd, even, 1)
+    sides = swap(sides)
+    blocks = lax.axis_size("wall")
+    odd = lax.ppermute(odd, "wall", pairs(blocks, 1, 1))
+    even = lax.ppermute(even, "wall", pairs(blocks, 1, 0))
 
     stream, wall = pl.pallas_call(
         stream_kernel,
@@ -474,19 +505,24 @@
         name="streamwise",
     )(field, sides, in_hbm(wall_source))
 
-    rate, work, total, *sent = pl.pallas_call(
+    rate, work, total, keep, give = pl.pallas_call(
         sweep_kernel,
         in_specs=[VMEM] * 8,
-        out_specs=[VMEM] * 7,
-        out_shape=[resident, resident, pltpu.VMEM((2, planes, 8, 128), f32)] + [rows] * 4,
+        out_specs=[VMEM] * 5,
+        out_shape=[resident, resident, pltpu.VMEM((2, planes, 8, 128), f32), pltpu.VMEM((2, planes, 8, 128), f32), ends],
         compiler_params=params(2),
         name="sweeps",
     )(coef, fading, field, stream, wall, own, odd, even)
 
-    odd1, even1, odd2, even2 = sent
-    far = exchange(odd2, even2, 2)
-    near = exchange(odd1, even1, 1)
-    arrived = [*near, *far]
+    odd, even = pl.pallas_call(
+        pack_kernel,
+        in_specs=[VMEM] * 2,
+        out_specs=[VMEM] * 2,
+        out_shape=[ends] * 2,
+        compiler_params=params(2),
+        name="pack",
+    )(keep, swap(give))
+    odd, even = carried(odd, 1), carried(even, 0)
 
     tendency, partial = pl.pallas_call(
         settle_kernel,
@@ -498,6 +534,8 @@
         cost_estimate=pl.CostEstimate(flops=4_000_000_000, transcendentals=0, bytes_accessed=0),
         name="settle",
     )(coef, field, work, rate)
+    odd, even, partial = lax.optimization_barrier((odd, even, partial))
+    arrived = [odd, even, swap(odd), swap(even)]
 
     advanced = pl.pallas_call(
         finish_kernel,

time: 44.5 us -> 41.8 us (0.939); the launches traced: 44.4 us -> 41.1 us
  starting transfers between devices: 18.8 us -> 14.1 us
  waiting for transfers between devices: 1.67 us -> 3.34 us
    ppermute x7 -> x8, starting transfers between devices: 18.8 us -> 14.1 us  [the longest x1 6.96 us: on_device(): odd = lax.ppermute(odd, 'wall', pairs(blocks, 1, 1))]
    ppermute x7 -> x8, waiting for transfers between devices: 1.67 us -> 3.34 us  [the longest x2 1.57 us: carried(): return lax.ppermute(x, ('wall', 'stream'), moves)]
    pallas_call x1 -> x2, Pallas kernels: 5.1 us -> 5.04 us  [the longest x1 5.03 us: on_device(): pl.pallas_call(sweep_kernel, in_specs=[VMEM] * 8, out_specs=[VMEM] * 5, o...]
  transfers between devices with their start and end apart: 7 -> 8, of which waited for: 2 -> 5; matrix products, arithmetic and copies ran while one was open for 0% -> 0% of each run, Pallas kernels for 19% -> 20%
where the time goes in v3:
time: 41.8 us; the launch traced here: 41.1 us
  Pallas kernels  21.9 us (52%)
  starting transfers between devices  14.1 us (34%)
  waiting for transfers between devices  3.34 us (8%)
  between operations  1.55 us (4%)
    ppermute x1, starting transfers between devices, on_device(): odd = lax.ppermute(odd, 'wall', pairs(blocks, 1, 1))  6.96 us
    ppermute x2, starting transfers between devices, carried(): return lax.ppermute(x, ('wall', 'stream'), moves)  6.4 us
    pallas_call x1, Pallas kernels, on_device(): pl.pallas_call(sweep_kernel, in_specs=[VMEM] * 8, out_specs=[VMEM] * 5, o...  5.03 us
    pallas_call x1, Pallas kernels, on_device(): pl.pallas_call(edges_kernel, in_specs=[ANY, ANY], out_specs=[VMEM] * 7 +...  4.68 us
    pallas_call x1, Pallas kernels, on_device(): pl.pallas_call(stream_kernel, in_specs=[VMEM, VMEM, ANY], out_specs=[VMEM...  4.28 us
    pallas_call x1, Pallas kernels, on_device(): pl.pallas_call(finish_kernel, in_specs=[VMEM] * 8, out_specs=ANY, out_sha...  4.13 us
    pallas_call x1, Pallas kernels, on_device(): pl.pallas_call(settle_kernel, in_specs=[VMEM] * 4, out_specs=[ANY, VMEM],...  3.8 us
    ppermute x2, waiting for transfers between devices, carried(): return lax.ppermute(x, ('wall', 'stream'), moves)  1.57 us
  transfers between devices with their start and end apart: 8, of which 5 were waited for; matrix products, arithmetic and copies ran while one was open for 0% of the time, Pallas kernels for 20%

profile of v3, /device:TPU:96, one launch (start us, length us, event | category | flops | bytes accessed | tf_op | source)
XLA Modules:
  0.0 41.1 jit_solution(7285664467338240813)
XLA Ops:
  0.6 4.7 %edges.1 = (f32[10,24,8,8,128]{4,3,2,1,0:T(8,128)S(1)}, f32[2,10,24,8,128]{4,3,2,1,0:T(8,128)S(1)}, f32[2,2,10,8,128]{4,3,2,1,0:T(8,128)S(1)}, f32[2,10,8,128]{3...) custom-call(f32[10,24,8,8,1,128]{5,4,3,2,1,0:T(1,128)} %bitcast.22, ...), custom_call_target="tpu_custom_call" | custom-call | tf_op jit(solution)/shard_map/edges/pallas_call | solution.py:474
  5.3 0.1 collective-permute-start.2
  5.4 7.0 %collective-permute-start.3 = (f32[2,10,8,128]{3,2,1,0:T(8,128)S(1)}, f32[2,10,8,128]{3,2,1,0:T(8,128)S(1)}, u32[]{:S(2)}, u32[]{:S(2)}) collective-permute-start(f32[2,10,8,128]{3,2,1,0:T(8,128)S(1)} %get-tuple-element.105), channel_id=1, source_target_pairs={{2,4},{4,2},{6,8},{8,6},{10,12},{12,10},{14,16},{16,14},{18,20},{2... | collective-permute-start | bytes 245768 | tf_op jit(solution)/shard_map/ppermute | solution.py:494
  12.4 0.1 collective-permute-start.4
  12.5 0.0 collective-permute-done.2.sides
  12.5 4.3 %streamwise.1 = (f32[10,24,8,8,128]{4,3,2,1,0:T(8,128)S(1)}, f32[2,24,8,8,128]{4,3,2,1,0:T(8,128)S(1)}) custom-call(f32[10,24,8,8,128]{4,3,2,1,0:T(8,128)S(1)} %get-tuple-element.99.field, f32[2,10,24,8,128]{4,3,2,1,0:T(8,128)S(1)} %collective-permute-done.2.sides, f32[2,24,8,8,1,128]{5,4,3,2,1,0:T(1,128)} %bitcast.24), custom_call_target="tpu_custom_call" | custom-call | flops 4000000000 | tf_op jit(solution)/shard_map/streamwise/pallas_call | solution.py:497
  16.8 0.0 collective-permute-done.3.odd_in
  16.8 0.2 collective-permute-done.4.even_in
  17.0 5.0 %sweeps.1 = (f32[10,24,8,8,128]{4,3,2,1,0:T(8,128)S(1)}, f32[10,24,8,8,128]{4,3,2,1,0:T(8,128)S(1)}, f32[2,10,8,128]{3,2,1,0:T(8,128)S(1)}, f32[2,10,8,128]{3,2,1,0:T(8,128)S(1)}, f32[2,10,8,128]{3,2,1,0:T(8,128)S(1)}) custom-call(f32[5,6,8,128]{3,2,1,0:T(8,128)S(1)} %get-tuple-element.98.coef, f32[5,24,8,128]{3,2,1,0:T(8,128)S(1)} %get-tuple-element.100.fading, ...), custom_call_target="tpu_custom_call" | custom-call | tf_op jit(solution)/shard_map/sweeps/pallas_call | solution.py:508
  22.0 0.1 collective-permute-start.5
  22.1 1.3 %collective-permute-done.5.got = f32[2,10,8,128]{3,2,1,0:T(8,128)S(1)} collective-permute-done((f32[2,10,8,128]{3,2,1,0:T(8,128)S(1)}, f32[2,10,8,128]{3,2,1,0:T(8,128)S(1)}, u32[]{:S(2)}, u32[]{:S(2)}) %collective-permute-start.5) | collective-permute-done | bytes 81952 | tf_op jit(solution)/shard_map/ppermute | solution.py:417
  23.4 6.3 %collective-permute-start.6 = (f32[2,10,8,128]{3,2,1,0:T(8,128)S(1)}, f32[2,10,8,128]{3,2,1,0:T(8,128)S(1)}, u32[]{:S(2)}, u32[]{:S(2)}) collective-permute-start(f32[2,10,8,128]{3,2,1,0:T(8,128)S(1)} %get-tuple-element.113), channel_id=1, source_target_pairs={{2,4},{4,2},{6,8},{8,6},{10,12},{12,10},{14,16},{16,14},{18,20},{2... | collective-permute-start | bytes 245768 | tf_op jit(solution)/shard_map/ppermute | solution.py:423
  29.7 0.1 collective-permute-start.7
  29.8 3.8 %settle.1 = (f32[10,24,8,8,1,128]{5,4,3,2,1,0:T(1,128)}, f32[10,24,8,8,128]{4,3,2,1,0:T(8,128)S(1)}) custom-call(f32[5,6,8,128]{3,2,1,0:T(8,128)S(1)} %get-tuple-element.98.coef, f32[10,24,8,8,128]{4,3,2,1,0:T(8,128)S(1)} %get-tuple-element.99.field, f32[10,24,8,8,128]{4,3,2,1,0:T(8,128)S(1)} %get-tuple-element.107.work, ...), custom_call_target="tpu_custom_call" | custom-call | flops 4000000000 | tf_op jit(solution)/shard_map/settle/pallas_call | solution.py:527
  33.6 1.6 %collective-permute-done.6.odd_own = f32[2,10,8,128]{3,2,1,0:T(8,128)S(1)} collective-permute-done((f32[2,10,8,128]{3,2,1,0:T(8,128)S(1)}, f32[2,10,8,128]{3,2,1,0:T(8,128)S(1)}, u32[]{:S(2)}, u32[]{:S(2)}) %collective-permute-start.6) | collective-permute-done | bytes 81952 | tf_op jit(solution)/shard_map/ppermute | solution.py:423
  35.2 0.0 collective-permute-done.7.even_own
  35.2 0.0 collective-permute-start.8
  35.2 0.5 %collective-permute-start.9 = (f32[2,10,8,128]{3,2,1,0:T(8,128)S(1)}, f32[2,10,8,128]{3,2,1,0:T(8,128)S(1)}, u32[]{:S(2)}, u32[]{:S(2)}) collective-permute-start(f32[2,10,8,128]{3,2,1,0:T(8,128)S(1)} %collective-permute-done.7.even_own), channel_id=1, source_target_pairs={{0,1},{1,0},{2,3},{3,2},{4,5},{5,4},{6,7},{7,6},{8,9},{9,8},{10,11... | collective-permute-start | bytes 245768 | tf_op jit(solution)/shard_map/ppermute | solution.py:417
  36.4 0.1 collective-permute-done.8.odd_other
  36.5 0.2 collective-permute-done.9.even_other
  36.6 4.1 %finish.1 = f32[10,24,8,8,1,128]{5,4,3,2,1,0:T(1,128)} custom-call(f32[5,6,8,128]{3,2,1,0:T(8,128)S(1)} %get-tuple-element.98.coef, f32[5,24,8,128]{3,2,1,0:T(8,128)S(1)} %get-tuple-element.100.fading, f32[10,24,8,8,128]{4,3,2,1,0:T(8,128)S(1)} %get-tuple-element.116.partial, f32[2,10,8,128]{3,2,1,0:T(8,128)S(1)} %get-tuple-element.117.total, ...), custom_call_target="tpu_custom_call" | custom-call | tf_op jit(solution)/shard_map/finish/pallas_call | solution.py:540
  40.8 0.2 conditional.1
  (1 shorter events, 0.0 us)
Async XLA Ops:
  5.3 7.2 %collective-permute-start.2 = (f32[2,10,24,8,128]{4,3,2,1,0:T(8,128)S(1)}, f32[2,10,24,8,128]{4,3,2,1,0:T(8,128)S(1)}, u32[]{:S(2)}, u32[]{:S(2)}) collective-permute-start(f32[2,10,24,8,128]{4,3,2,1,0:T(8,128)S(1)} %get-tuple-element.101), channel_id=1, source_target_pairs={{0,1},{1,0},{2,3},{3,2},{4,5},{5,4},{6,7},{7,6},{8,9},{9,8},{10,11... | collective-permute-start | bytes 5898248 | tf_op jit(solution)/shard_map/ppermute | solution.py:417
  5.4 11.4 %collective-permute-start.3 = (f32[2,10,8,128]{3,2,1,0:T(8,128)S(1)}, f32[2,10,8,128]{3,2,1,0:T(8,128)S(1)}, u32[]{:S(2)}, u32[]{:S(2)}) collective-permute-start(f32[2,10,8,128]{3,2,1,0:T(8,128)S(1)} %get-tuple-element.105), channel_id=1, source_target_pairs={{2,4},{4,2},{6,8},{8,6},{10,12},{12,10},{14,16},{16,14},{18,20},{2... | collective-permute-start | bytes 245768 | tf_op jit(solution)/shard_map/ppermute | solution.py:494
  12.4 4.6 %collective-permute-start.4 = (f32[2,10,8,128]{3,2,1,0:T(8,128)S(1)}, f32[2,10,8,128]{3,2,1,0:T(8,128)S(1)}, u32[]{:S(2)}, u32[]{:S(2)}) collective-permute-start(f32[2,10,8,128]{3,2,1,0:T(8,128)S(1)} %get-tuple-element.106), channel_id=1, source_target_pairs={{0,2},{2,0},{4,6},{6,4},{8,10},{10,8},{12,14},{14,12},{16,18},{18,... | collective-permute-start | bytes 245768 | tf_op jit(solution)/shard_map/ppermute | solution.py:495
  22.0 1.4 %collective-permute-start.5 = (f32[2,10,8,128]{3,2,1,0:T(8,128)S(1)}, f32[2,10,8,128]{3,2,1,0:T(8,128)S(1)}, u32[]{:S(2)}, u32[]{:S(2)}) collective-permute-start(f32[2,10,8,128]{3,2,1,0:T(8,128)S(1)} %get-tuple-element.112), channel_id=1, source_target_pairs={{0,1},{1,0},{2,3},{3,2},{4,5},{5,4},{6,7},{7,6},{8,9},{9,8},{10,11... | collective-permute-start | bytes 245768 | tf_op jit(solution)/shard_map/ppermute | solution.py:417
  23.4 11.8 %collective-permute-start.6 = (f32[2,10,8,128]{3,2,1,0:T(8,128)S(1)}, f32[2,10,8,128]{3,2,1,0:T(8,128)S(1)}, u32[]{:S(2)}, u32[]{:S(2)}) collective-permute-start(f32[2,10,8,128]{3,2,1,0:T(8,128)S(1)} %get-tuple-element.113), channel_id=1, source_target_pairs={{2,4},{4,2},{6,8},{8,6},{10,12},{12,10},{14,16},{16,14},{18,20},{2... | collective-permute-start | bytes 245768 | tf_op jit(solution)/shard_map/ppermute | solution.py:423
  29.7 5.5 %collective-permute-start.7 = (f32[2,10,8,128]{3,2,1,0:T(8,128)S(1)}, f32[2,10,8,128]{3,2,1,0:T(8,128)S(1)}, u32[]{:S(2)}, u32[]{:S(2)}) collective-permute-start(f32[2,10,8,128]{3,2,1,0:T(8,128)S(1)} %get-tuple-element.114), channel_id=1, source_target_pairs={{0,2},{2,0},{4,6},{6,4},{8,10},{10,8},{12,14},{14,12},{16,18},{18,... | collective-permute-start | bytes 245768 | tf_op jit(solution)/shard_map/ppermute | solution.py:423
  35.2 1.3 %collective-permute-start.8 = (f32[2,10,8,128]{3,2,1,0:T(8,128)S(1)}, f32[2,10,8,128]{3,2,1,0:T(8,128)S(1)}, u32[]{:S(2)}, u32[]{:S(2)}) collective-permute-start(f32[2,10,8,128]{3,2,1,0:T(8,128)S(1)} %collective-permute-done.6.odd_own), channel_id=1, source_target_pairs={{0,1},{1,0},{2,3},{3,2},{4,5},{5,4},{6,7},{7,6},{8,9},{9,8},{10,11... | collective-permute-start | bytes 245768 | tf_op jit(solution)/shard_map/ppermute | solution.py:417
  35.2 1.4 %collective-permute-start.9 = (f32[2,10,8,128]{3,2,1,0:T(8,128)S(1)}, f32[2,10,8,128]{3,2,1,0:T(8,128)S(1)}, u32[]{:S(2)}, u32[]{:S(2)}) collective-permute-start(f32[2,10,8,128]{3,2,1,0:T(8,128)S(1)} %collective-permute-done.7.even_own), channel_id=1, source_target_pairs={{0,1},{1,0},{2,3},{3,2},{4,5},{5,4},{6,7},{7,6},{8,9},{9,8},{10,11... | collective-permute-start | bytes 245768 | tf_op jit(solution)/shard_map/ppermute | solution.py:417
